TPU v7x, 16 devices: a whole 2x2x2 slice. The times are simulated.
16 devices in a mesh: dp: 4 (over z, y), tp: 4 (over x, core).
Axes of the slice: x: 2, y: 2, z: 2, core: 2. Of those that a mesh axis runs over, the one named last changes fastest.
Arguments:
- x_in: bfloat16 [16, 64, 5120], P('dp'), parts along dimension 0
- start_pos: int32 [16], P('dp'), parts along dimension 0
- kv_state: float32 [16, 20, 256, 512], P('dp', 'tp'), parts along dimension 0
- ln1_gain: float32 [5120], replicated
- ln1_bias: float32 [5120], replicated
- w_q: bfloat16 [5120, 5120], P(None, 'tp')
- w_k: bfloat16 [5120, 5120], P(None, 'tp')
- w_v: bfloat16 [5120, 10240], P(None, 'tp')
- w_g: bfloat16 [5120, 10240], P(None, 'tp')
- w_o: bfloat16 [10240, 5120], P('tp')
- ln2_gain: float32 [5120], replicated
- ln2_bias: float32 [5120], replicated
- w_up: bfloat16 [5120, 10240], P(None, 'tp')
- w_down: bfloat16 [10240, 5120], P('tp')
Outputs:
- output 1: bfloat16 [16, 64, 5120], P('dp'), parts along dimension 0
- output 2: float32 [16, 20, 256, 512], P('dp', 'tp'), parts along dimension 0
There are 4 independent parts. A program takes and returns all parts, laid end to end along the dimension named above; an argument that names none is the same for every part.
All inputs are finite; a program needn't handle non-finite values.
Results may differ from a plain program's by a relative error of at most 0.0131123.
Values are sent between devices in bfloat16 or wider.
A program may use at most 1 GiB of HBM per device.

v0:
```python
import jax
import jax.numpy as jnp
from jax import lax
from jax.sharding import PartitionSpec as P

NORM_EPS = 1e-5
GROUP_EPS = 1e-6
ROPE_BASE = 10000.0


def layer_norm(x_f32, norm_gain, norm_bias):
    row_mean = jnp.mean(x_f32, axis=-1, keepdims=True)
    centered = x_f32 - row_mean
    variance = jnp.mean(centered * centered, axis=-1, keepdims=True)
    return centered * lax.rsqrt(variance + NORM_EPS) * norm_gain + norm_bias


def rotate_half(head_vecs, cos_t, sin_t):
    half_dim = head_vecs.shape[-1] // 2
    first_half = head_vecs[..., :half_dim]
    second_half = head_vecs[..., half_dim:]
    return jnp.concatenate([first_half * cos_t - second_half * sin_t, second_half * cos_t + first_half * sin_t], axis=-1)


def rope_tables(first_pos, chunk_len, key_dim):
    half_dim = key_dim // 2
    inv_freq = jnp.power(ROPE_BASE, -jnp.arange(half_dim).astype(jnp.float32) / half_dim)
    positions = (first_pos[:, None] + jnp.arange(chunk_len)[None, :]).astype(jnp.float32)
    angles = positions[:, :, None] * inv_freq
    return jnp.cos(angles)[:, :, None, :], jnp.sin(angles)[:, :, None, :]


def head_log_decay(head_ids):
    return jnp.log1p(-jnp.exp2(-5.0 - head_ids.astype(jnp.float32)))


def project_heads(h_one, cos_t, sin_t, w_q, w_k, w_v, w_g, num_heads):
    d_model = h_one.shape[-1]
    key_dim = w_q.shape[1] // num_heads
    val_dim = w_v.shape[1] // num_heads
    q_raw = jnp.einsum('bcd,dhk->bchk', h_one, w_q.reshape(d_model, num_heads, key_dim), preferred_element_type=jnp.float32)
    k_raw = jnp.einsum('bcd,dhk->bchk', h_one, w_k.reshape(d_model, num_heads, key_dim), preferred_element_type=jnp.float32)
    queries = rotate_half(q_raw, cos_t, sin_t).astype(jnp.bfloat16)
    keys = (rotate_half(k_raw, cos_t, sin_t) * key_dim ** -0.5).astype(jnp.bfloat16)
    values = jnp.einsum('bcd,dhe->bche', h_one, w_v.reshape(d_model, num_heads, val_dim), preferred_element_type=jnp.float32).astype(jnp.bfloat16)
    gates = jnp.einsum('bcd,dhe->bche', h_one, w_g.reshape(d_model, num_heads, val_dim), preferred_element_type=jnp.float32)
    return queries, keys, values, gates


def mix_heads(queries, keys, values_f32, gates, state_in, log_gamma, w_o):
    chunk_len = queries.shape[1]
    num_heads = queries.shape[2]
    val_dim = values_f32.shape[3]
    step_ids = jnp.arange(chunk_len)
    step_gap = step_ids[:, None] - step_ids[None, :]
    inner_decay = jnp.where(step_gap[None] >= 0, jnp.exp(jnp.maximum(step_gap, 0).astype(jnp.float32)[None] * log_gamma[:, None, None]), 0.0)
    query_decay = jnp.exp((step_ids + 1).astype(jnp.float32)[:, None] * log_gamma[None, :])
    scores = jnp.einsum('bchk,bjhk->bhcj', queries, keys, preferred_element_type=jnp.float32) * inner_decay
    retained = jnp.einsum('bhcj,bjhe->bche', scores, values_f32) + jnp.einsum('bchk,bhke->bche', queries.astype(jnp.float32), state_in) * query_decay[:, :, None]
    row_mean = jnp.mean(retained, axis=-1, keepdims=True)
    centered = retained - row_mean
    variance = jnp.mean(centered * centered, axis=-1, keepdims=True)
    normed = centered * lax.rsqrt(variance + GROUP_EPS)
    mixed = (jax.nn.silu(gates) * normed).astype(jnp.bfloat16)
    return jnp.einsum('bche,hed->bcd', mixed, w_o.reshape(num_heads, val_dim, w_o.shape[1]), preferred_element_type=jnp.float32)


def chunk_state(keys, values_f32, log_gamma):
    chunk_len = keys.shape[1]
    step_ids = jnp.arange(chunk_len)
    key_decay = jnp.exp((chunk_len - 1 - step_ids).astype(jnp.float32)[:, None] * log_gamma[None, :])
    return jnp.einsum('bjhk,bjhe->bhke', keys.astype(jnp.float32) * key_decay[:, :, None], values_f32)


def feed_forward(x_mid, ln2_gain, ln2_bias, w_up, w_down):
    h_two = layer_norm(x_mid.astype(jnp.float32), ln2_gain, ln2_bias).astype(jnp.bfloat16)
    activated = jax.nn.gelu(jnp.einsum('bcd,df->bcf', h_two, w_up, preferred_element_type=jnp.float32), approximate=False).astype(jnp.bfloat16)
    return jnp.einsum('bcf,fd->bcd', activated, w_down, preferred_element_type=jnp.float32)


def solution(mesh):
    def local_layer(x_in, start_pos, kv_state, ln1_gain, ln1_bias, w_q, w_k, w_v, w_g, w_o, ln2_gain, ln2_bias, w_up, w_down):
        local_heads = kv_state.shape[1]
        chunk_len = x_in.shape[1]
        head_ids = lax.axis_index('tp') * local_heads + jnp.arange(local_heads)
        log_gamma = head_log_decay(head_ids)
        x_f32 = x_in.astype(jnp.float32)
        h_one = layer_norm(x_f32, ln1_gain, ln1_bias).astype(jnp.bfloat16)
        cos_t, sin_t = rope_tables(start_pos, chunk_len, kv_state.shape[2])
        queries, keys, values, gates = project_heads(h_one, cos_t, sin_t, w_q, w_k, w_v, w_g, local_heads)
        values_f32 = values.astype(jnp.float32)
        attn_part = mix_heads(queries, keys, values_f32, gates, kv_state, log_gamma, w_o).astype(jnp.bfloat16)
        new_state = jnp.exp(chunk_len * log_gamma)[:, None, None] * kv_state + chunk_state(keys, values_f32, log_gamma)
        attn_out = lax.psum(attn_part, 'tp')
        x_mid = (x_f32 + attn_out.astype(jnp.float32)).astype(jnp.bfloat16)
        ffn_part = feed_forward(x_mid, ln2_gain, ln2_bias, w_up, w_down).astype(jnp.bfloat16)
        ffn_out = lax.psum(ffn_part, 'tp')
        x_out = (x_mid.astype(jnp.float32) + ffn_out.astype(jnp.float32)).astype(jnp.bfloat16)
        return x_out, new_state

    in_specs = (P('dp', None, None), P('dp'), P('dp', 'tp', None, None), P(), P(), P(None, 'tp'), P(None, 'tp'), P(None, 'tp'), P(None, 'tp'), P('tp', None), P(), P(), P(None, 'tp'), P('tp', None))
    out_specs = (P('dp', None, None), P('dp', 'tp', None, None))
    return jax.shard_map(local_layer, mesh=mesh, in_specs=in_specs, out_specs=out_specs, check_vma=False)
```

profile of v0, /device:TPU:0, one launch (start us, length us, event | category | flops | bytes accessed | tf_op | source)
XLA Modules:
  0.0 353.8 jit_solution(9857833602381346558)
XLA Ops:
  7.2 0.0 all-reduce.3.cloned.1.call-start
  7.3 2.3 convert_reduce_fusion.1
  9.6 0.1 copy-done
  9.7 0.8 fusion.16
  10.5 17.6 %copy.26 = bf16[5120,1280]{0,1:T(8,128)(2,1)} copy(bf16[5120,1280]{1,0:T(8,128)(2,1)} %param.20) | data formatting | bytes 26214400 | tf_op args[6]
  28.2 17.6 %copy.24 = bf16[5120,1280]{0,1:T(8,128)(2,1)} copy(bf16[5120,1280]{1,0:T(8,128)(2,1)} %param.19) | data formatting | bytes 26214400 | tf_op args[5]
  45.8 9.7 %fusion.129 = f32[4,64,5,256]{3,1,2,0:T(8,128)} fusion(bf16[5120,5,256,1]{0,2,1,3:T(8,128)(2,1)} %bitcast.65, bf16[4,64,5120]{2,1,0:T(8,128)(2,1)S(1)} %copy-done, f32[5120]{0:T(1024)S(1)} %copy-done.5, f32[5120]{0:T(1024)S(1)} %copy-done.6, f32[4,64]{1,0:T(4,128)S(1)} %add_rsqrt_fusion.2, f32[4,64]{1,0:T(4,128)S(1)} %broadcast_multiply_fusion.2), kind=kOutput, calls=%fused_computation.170 | convolution fusion | flops 3363307520 | bytes 17082368 | tf_op jit(solution)/shard_map/bcd,dhk->bchk/dot_general | solution.py:42
  55.5 9.7 %fusion.131 = f32[4,64,5,256]{3,1,2,0:T(8,128)} fusion(bf16[5120,5,256,1]{0,2,1,3:T(8,128)(2,1)} %bitcast.64, bf16[4,64,5120]{2,1,0:T(8,128)(2,1)S(1)} %copy-done, f32[5120]{0:T(1024)S(1)} %copy-done.5, f32[5120]{0:T(1024)S(1)} %copy-done.6, f32[4,64]{1,0:T(4,128)S(1)} %add_rsqrt_fusion.2, f32[4,64]{1,0:T(4,128)S(1)} %broadcast_multiply_fusion.2), kind=kOutput, calls=%fused_computation.171 | convolution fusion | flops 3363307520 | bytes 17082368 | tf_op jit(solution)/shard_map/bcd,dhk->bchk/dot_general | solution.py:41
  65.2 0.1 add_convert_fusion.1
  65.3 35.1 %copy.22 = bf16[5120,2560]{0,1:T(8,128)(2,1)} copy(bf16[5120,2560]{1,0:T(8,128)(2,1)} %param.21) | data formatting | bytes 52428800 | tf_op args[7]
  100.5 13.5 %convolution_convert_fusion = bf16[4,64,5,512]{3,1,2,0:T(8,128)(2,1)} fusion(bf16[5120,5,512,1]{0,2,1,3:T(8,128)(2,1)} %bitcast.63, bf16[4,64,5120]{2,1,0:T(8,128)(2,1)S(1)} %copy-done, f32[5120]{0:T(1024)S(1)} %copy-done.5, f32[5120]{0:T(1024)S(1)} %copy-done.6, f32[4,64]{1,0:T(4,128)S(1)} %add_rsqrt_fusion.2, f32[4,64]{1,0:T(4,128)S(1)} %broadcast_multiply_fusion.2), kind=kOutput, calls=%fused_computation.60 | convolution fusion | flops 6719406080 | bytes 30189568 | tf_op jit(solution)/shard_map/bcd,dhe->bche/dot_general | solution.py:45
  113.9 0.5 multiply_cosine_fusion
  114.5 0.1 exponential_select_fusion
  114.6 0.1 multiply_exponential_fusion
  114.7 3.1 multiply_subtract_fusion
  117.8 3.8 %fusion.77 = f32[4,5,512,64]{2,3,1,0:T(8,128)} fusion(bf16[4,64,5,512]{3,1,2,0:T(8,128)(2,1)} %convolution_convert_fusion, bf16[4,64,5,128]{3,1,2,0:T(8,128)(2,1)} %get-tuple-element.10, bf16[4,64,5,128]{3,1,2,0:T(8,128)(2,1)} %get-tuple-element.11, f32[5,64,64]{2,1,0:T(8,128)S(1)} %exponential_select_fusion, f32[4,64,5,128]{3,1,2,0:T(8,128)} %get-tuple-element.7, ...), kind=kOutput, calls=%fused_computation.100 | convolution fusion | flops 128204800 | bytes 5980160 | tf_op jit(solution)/shard_map/bhcj,bjhe->bche/dot_general | solution.py:59
  121.6 6.1 %fusion.137 = (f32[4,64,5]{1,2,0:T(8,128)S(1)}, f32[4,64,5,512]{3,1,2,0:T(8,128)S(1)}) fusion(f32[64,5]{0,1:T(8,128)S(1)} %get-tuple-element.15, f32[4,5,256,512]{3,2,1,0:T(8,128)} %param.16, bf16[4,64,5,128]{3,1,2,0:T(8,128)(2,1)} %get-tuple-element.10, bf16[4,64,5,128]{3,1,2,0:T(8,128)(2,1)} %get-tuple-element.11, f32[4,5,512,64]{2,3,1,0:T(8,128)} %fusion.77), kind=kOutput, calls=%fused_computation.172 | convolution fusion | flops 338819840 | bytes 16390400 | tf_op jit(solution)/shard_map/bchk,bhke->bche/dot_general | solution.py:59
  127.8 1.5 copy-done.3
  129.3 0.5 multiply_reduce_fusion
  129.8 35.2 %copy.20 = bf16[5120,2560]{0,1:T(8,128)(2,1)} copy(bf16[5120,2560]{1,0:T(8,128)(2,1)} %param.22) | data formatting | bytes 52428800 | tf_op args[8]
  165.0 14.1 %multiply_convert_fusion.clone.4 = bf16[4,64,5,512]{3,1,2,0:T(8,128)(2,1)} fusion(bf16[5120,5,512,1]{0,2,1,3:T(8,128)(2,1)} %bitcast.62, f32[4,64,5,512]{3,1,2,0:T(8,128)} %copy-done.3, f32[4,64,5]{1,2,0:T(8,128)S(1)} %add_rsqrt_fusion, f32[4,64,5]{1,2,0:T(8,128)S(1)} %broadcast_multiply_fusion, bf16[4,64,5120]{2,1,0:T(8,128)(2,1)S(1)} %copy-done, ...), kind=kOutput, calls=%fused_computation.57.clone.clone.clone.1 | convolution fusion | flops 6723993600 | bytes 32821248 | tf_op jit(solution)/shard_map/bcd,dhe->bche/dot_general | solution.py:46
  179.1 13.7 %fusion.4 = bf16[4,64,5120]{2,1,0:T(8,128)(2,1)} fusion(bf16[5,512,5120,1]{2,1,0,3:T(8,128)(2,1)} %bitcast.66, bf16[4,64,5,512]{3,1,2,0:T(8,128)(2,1)} %multiply_convert_fusion.clone.4), kind=kOutput, calls=%fused_computation.12 | convolution fusion | flops 6712197120 | bytes 30146560 | tf_op jit(solution)/shard_map/bche,hed->bcd/dot_general | solution.py:65
  192.8 0.0 all-reduce.5.cloned.1.call-start
  192.8 58.9 %all-reduce.3.cloned.1.call-done = bf16[4,64,5120]{2,1,0:T(8,128)(2,1)} async-done(((bf16[4,64,5120]{2,1,0:T(8,128)(2,1)}), bf16[4,64,5120]{2,1,0:T(8,128)(2,1)}) %all-reduce.3.cloned.1.call-update) | async-done | bytes 2621456 | tf_op jit(solution)/shard_map/psum | solution.py:94
  251.8 2.8 convert_reduce_fusion
  254.6 0.8 fusion.12
  255.4 13.4 %fusion.80 = (u8[64,2560]{1,0:T(8,128)(4,1)S(1)}, u8[64,2560]{1,0:T(8,128)(4,1)S(1)}, f32[4,64,2560]{2,1,0:T(8,128)S(1)}) fusion(bf16[5120,2560]{1,0:T(8,128)(2,1)} %param.26, bf16[4,64,5120]{2,1,0:T(8,128)(2,1)S(1)} %get-tuple-element.5, f32[5120]{0:T(1024)S(1)} %copy-done.7, f32[5120]{0:T(1024)S(1)} %copy-done.8, f32[4,64]{1,0:T(4,128)S(1)} %add_rsqrt_fusion.1, ...), kind=kOutput, calls=%fused_computation.108 | convolution fusion | flops 6726942720 | bytes 31827968 | tf_op jit(solution)/shard_map/bcd,df->bcf/dot_general | solution.py:77
  268.8 17.6 %fusion.5 = bf16[4,64,5120]{2,1,0:T(8,128)(2,1)} fusion(bf16[2560,5120]{1,0:T(8,128)(2,1)} %param.27, f32[4,64,2560]{2,1,0:T(8,128)S(1)} %get-tuple-element.18, u8[64,2560]{1,0:T(8,128)(4,1)S(1)} %get-tuple-element.3, u8[64,2560]{1,0:T(8,128)(4,1)S(1)} %get-tuple-element.2), kind=kOutput, calls=%fused_computation.13 | convolution fusion | flops 6758072320 | bytes 31784960 | tf_op jit(solution)/shard_map/bcf,fd->bcd/dot_general | solution.py:78
  286.4 0.0 all-reduce.5.cloned.1.call-update
  286.5 11.1 %multiply_add_fusion = f32[4,5,256,512]{3,2,1,0:T(8,128)} fusion(f32[4,5,256,512]{3,2,1,0:T(8,128)} %param.16, f32[5]{0:T(128)S(1)} %multiply_exponential_fusion.2, bf16[4,64,5,512]{3,1,2,0:T(8,128)(2,1)} %convolution_convert_fusion, f32[64,5]{0,1:T(8,128)S(1)} %get-tuple-element.14, f32[4,64,5,128]{3,1,2,0:T(8,128)} %get-tuple-element.7, ...), kind=kOutput, calls=%fused_computation.4 | convolution fusion | flops 342425600 | bytes 23594260 | tf_op jit(solution)/shard_map/bjhk,bjhe->bhke/dot_general | solution.py:72
  297.6 45.1 %all-reduce.5.cloned.1.call-done = bf16[4,64,5120]{2,1,0:T(8,128)(2,1)} async-done(((bf16[4,64,5120]{2,1,0:T(8,128)(2,1)}), bf16[4,64,5120]{2,1,0:T(8,128)(2,1)}) %all-reduce.5.cloned.1.call-update) | async-done | bytes 2621456 | tf_op jit(solution)/shard_map/psum | solution.py:97
  342.7 4.2 %fusion.21 = bf16[4,64,5120]{2,1,0:T(8,128)(2,1)} fusion(bf16[4,64,5120]{2,1,0:T(8,128)(2,1)S(1)} %copy-done.2, bf16[4,64,5120]{2,1,0:T(8,128)(2,1)} %all-reduce.5.cloned.1.call-done), kind=kLoop, calls=%fused_computation.27 | loop fusion | flops 5242880 | bytes 7864320 | tf_op jit(solution)/shard_map/convert_element_type | solution.py:98
  (29 shorter events, 0.2 us)
Async XLA Ops:
  7.2 2.5 copy-start
  7.2 244.6 %all-reduce.3.cloned.1.call-start = ((), (), s32[]{:S(2)}) async-start(), calls=%async_computation | async-start | bytes 5242880 | tf_op jit(solution)/shard_map/psum | solution.py:94
  28.2 17.6 %copy-start.5 = (f32[5120]{0:T(1024)S(1)}, f32[5120]{0:T(1024)}, u32[]{:S(2)}) copy-start(f32[5120]{0:T(1024)} %param.18) | copy-start | bytes 61444
  28.2 17.6 %copy-start.6 = (f32[5120]{0:T(1024)S(1)}, f32[5120]{0:T(1024)}, u32[]{:S(2)}) copy-start(f32[5120]{0:T(1024)} %param.17) | copy-start | bytes 61444
  55.5 9.7 %copy-start.4 = (s32[4]{0:T(128)S(1)}, s32[4]{0:T(128)}, u32[]{:S(2)}) copy-start(s32[4]{0:T(128)} %param.15) | copy-start | bytes 52
  127.8 1.5 copy-start.3
  192.8 150.0 %all-reduce.5.cloned.1.call-start = ((), (), s32[]{:S(2)}) async-start(), calls=%async_computation.1 | async-start | bytes 5242880 | tf_op jit(solution)/shard_map/psum | solution.py:97
  254.5 14.3 %copy-start.1 = (bf16[4,64,5120]{2,1,0:T(8,128)(2,1)}, bf16[4,64,5120]{2,1,0:T(8,128)(2,1)S(1)}, u32[]{:S(2)}) copy-start(bf16[4,64,5120]{2,1,0:T(8,128)(2,1)S(1)} %get-tuple-element.5) | copy-start | bytes 7864324
  254.5 0.9 copy-start.7
  254.6 0.9 copy-start.8
  286.5 56.3 %copy-start.2 = (bf16[4,64,5120]{2,1,0:T(8,128)(2,1)S(1)}, bf16[4,64,5120]{2,1,0:T(8,128)(2,1)}, u32[]{:S(2)}) copy-start(bf16[4,64,5120]{2,1,0:T(8,128)(2,1)} %copy-done.1) | copy-start | bytes 7864324
Sparse Core Ops, SparseCore 0:
  192.9 58.8 all-reduce.2
  286.6 56.1 all-reduce.4
where the time goes:
time: 357 us; the launch traced here: 354 us
  matrix products  113 us (32%)
  local copies, waits for them, and re-layouts  107 us (30%)
  waiting for transfers between devices  104 us (29%)
  other arithmetic  15.5 us (4%)
  between operations  14.2 us (4%)
    unnamed x22, local copies, waits for them, and re-layouts  107 us
    psum x1, waiting for transfers between devices, local_layer(): attn_out = lax.psum(attn_part, 'tp')  58.9 us
    psum x1, waiting for transfers between devices, local_layer(): ffn_out = lax.psum(ffn_part, 'tp')  45.1 us
    dot_general x1, matrix products, feed_forward(): jnp.einsum('bcf,fd->bcd', activated, w_down, preferred_element_type=jnp.f...  17.6 us
    dot_general x1, matrix products, project_heads(): jnp.einsum('bcd,dhe->bche', h_one, w_g.reshape(d_model, num_heads, val_di...  14.1 us
    dot_general x1, matrix products, mix_heads(): jnp.einsum('bche,hed->bcd', mixed, w_o.reshape(num_heads, val_dim, w_o.sh...  13.7 us
    dot_general x1, matrix products, project_heads(): jnp.einsum('bcd,dhe->bche', h_one, w_v.reshape(d_model, num_heads, val_di...  13.5 us
    dot_general x1, matrix products, feed_forward(): jnp.einsum('bcd,df->bcf', h_two, w_up, preferred_element_type=jnp.float32)  13.4 us
  transfers between devices with their start and end apart: 2, of which 2 were waited for; matrix products, arithmetic and copies ran while one was open for 3% of the time, Pallas kernels for 0%

commit v1 on v0

v1 whole, which is shorter than its diff:
```python
import numpy as np
import jax
import jax.numpy as jnp
from jax import lax
from jax.experimental import pallas as pl
from jax.experimental.pallas import tpu as pltpu
from jax.sharding import PartitionSpec as P

NORM_EPS = 1e-5
GROUP_EPS = 1e-6
ROPE_BASE = 10000.0
BF = jnp.bfloat16
F32 = jnp.float32
MESH = pl.DeviceIdType.MESH


def layer_norm(x_f32, norm_gain, norm_bias):
    row_mean = jnp.mean(x_f32, axis=-1, keepdims=True)
    centered = x_f32 - row_mean
    variance = jnp.mean(centered * centered, axis=-1, keepdims=True)
    return centered * lax.rsqrt(variance + NORM_EPS) * norm_gain + norm_bias


def rope_tables(first_pos, chunk_len, key_dim):
    half_dim = key_dim // 2
    inv_freq = jnp.power(ROPE_BASE, -jnp.arange(half_dim).astype(F32) / half_dim)
    positions = (first_pos[:, None] + jnp.arange(chunk_len)[None, :]).astype(F32)
    angles = (positions[:, :, None] * inv_freq).reshape(-1, half_dim)
    return jnp.cos(angles), jnp.sin(angles)


def split2(val):
    high = val.astype(BF)
    return high, (val - high.astype(F32)).astype(BF)


def dot(lhs, rhs):
    return jnp.dot(lhs, rhs, preferred_element_type=F32)


def mix_kernel(lg_ref, x_hbm, cos_ref, sin_ref, g_ref, b_ref, wq, wk, wv, wg, s_hbm, z_hbm, so_hbm,
               xb, hb, wb, sb, sob, qb, kb, vb, gb, zb, xsem, wsem, ssem, sosem, zsem):
    heads = wq.shape[1] // 256
    nseq = s_hbm.shape[0]
    clen = x_hbm.shape[0] // nseq
    first_head = lax.axis_index('tp') * heads

    def wcopy(head, i):
        if i == 0:
            src = wq.at[:, pl.ds(pl.multiple_of(head * 256, 256), 256)]
        elif i == 1:
            src = wk.at[:, pl.ds(pl.multiple_of(head * 256, 256), 256)]
        elif i < 4:
            src = wv.at[:, pl.ds(pl.multiple_of(head * 512 + (i - 2) * 256, 256), 256)]
        else:
            src = wg.at[:, pl.ds(pl.multiple_of(head * 512 + (i - 4) * 256, 256), 256)]
        return pltpu.make_async_copy(src, wb.at[i], wsem.at[i])

    def scopy(head):
        slot = lax.rem(head, 2)
        return pltpu.make_async_copy(s_hbm.at[:, head], sb.at[slot], ssem.at[slot])

    def socopy(head):
        slot = lax.rem(head, 2)
        return pltpu.make_async_copy(sob.at[slot], so_hbm.at[:, head], sosem.at[slot])

    def zcopy(head):
        slot = lax.rem(head, 2)
        return pltpu.make_async_copy(zb.at[slot], z_hbm.at[:, pl.ds(pl.multiple_of(head * 512, 512), 512)], zsem.at[slot])

    xcopy = pltpu.make_async_copy(x_hbm, xb, xsem)
    xcopy.start()
    for i in range(3):
        wcopy(0, i).start()
    scopy(0).start()
    for i in range(3, 6):
        wcopy(0, i).start()
    xcopy.wait()

    def ln_rows(r, carry):
        rows = pl.ds(pl.multiple_of(r * 16, 16), 16)
        hb[rows, :] = layer_norm(xb[rows, :].astype(F32), g_ref[...], b_ref[...]).astype(BF)
        return carry
    lax.fori_loop(0, xb.shape[0] // 16, ln_rows, 0)

    step_i = lax.broadcasted_iota(jnp.int32, (clen, clen), 0)
    step_j = lax.broadcasted_iota(jnp.int32, (clen, clen), 1)
    gap = step_i - step_j
    tok_q = lax.broadcasted_iota(jnp.int32, (clen, 512), 0).astype(F32)
    tok_k = lax.broadcasted_iota(jnp.int32, (clen, 256), 0).astype(F32)

    def head_body(head, carry):
        def proj(i):
            wcopy(head, i).wait()
            res = dot(hb[...], wb[i])

            @pl.when(head + 1 < heads)
            def _():
                wcopy(head + 1, i).start()
            return res

        @pl.when(head + 1 < heads)
        def _():
            scopy(head + 1).start()

        cos_t = cos_ref[...]
        sin_t = sin_ref[...]
        res = proj(0)
        qb[:, :128] = (res[:, :128] * cos_t - res[:, 128:] * sin_t).astype(BF)
        qb[:, 128:] = (res[:, 128:] * cos_t + res[:, :128] * sin_t).astype(BF)
        res = proj(1)
        kb[:, :128] = ((res[:, :128] * cos_t - res[:, 128:] * sin_t) * 0.0625).astype(BF)
        kb[:, 128:] = ((res[:, 128:] * cos_t + res[:, :128] * sin_t) * 0.0625).astype(BF)
        vb[:, :256] = proj(2).astype(BF)
        vb[:, 256:] = proj(3).astype(BF)
        gb[:, :256] = proj(4)
        gb[:, 256:] = proj(5)

        log_g = lg_ref[first_head + head]
        inner_decay = jnp.where(gap >= 0, jnp.exp(jnp.maximum(gap, 0).astype(F32) * log_g), 0.0)
        query_decay = jnp.exp((tok_q + 1.0) * log_g)
        key_decay = jnp.exp((clen - 1.0 - tok_k) * log_g)
        state_decay = jnp.exp(jnp.full((1, 512), clen, F32) * log_g)
        slot = lax.rem(head, 2)
        scopy(head).wait()

        @pl.when(head >= 2)
        def _():
            socopy(head - 2).wait()
            zcopy(head - 2).wait()

        for s in range(nseq):
            rows = slice(s * clen, (s + 1) * clen)
            q, k, v = qb[rows, :], kb[rows, :], vb[rows, :]
            scores = lax.dot_general(q, k, (((1,), (1,)), ((), ())), preferred_element_type=F32) * inner_decay
            sc_hi, sc_lo = split2(scores)
            state = sb[slot, s]
            st_hi, st_lo = split2(state)
            out = dot(sc_hi, v) + dot(sc_lo, v) + (dot(q, st_hi) + dot(q, st_lo)) * query_decay
            mean = jnp.mean(out, axis=-1, keepdims=True)
            cent = out - mean
            var = jnp.mean(cent * cent, axis=-1, keepdims=True)
            gates = gb[rows, :]
            zb[slot, rows, :] = (gates * jax.nn.sigmoid(gates) * (cent * lax.rsqrt(var + GROUP_EPS))).astype(BF)
            kd_hi, kd_lo = split2(k.astype(F32) * key_decay)
            tdot = lambda a: lax.dot_general(a, v, (((0,), (0,)), ((), ())), preferred_element_type=F32)
            sob[slot, s] = state * state_decay + (tdot(kd_hi) + tdot(kd_lo))
        socopy(head).start()
        zcopy(head).start()
        return carry

    lax.fori_loop(0, heads, head_body, 0)
    for head in (heads - 2, heads - 1):
        socopy(head).wait()
        zcopy(head).wait()


def mix_call(x2d, cos_t, sin_t, gain, bias, w_q, w_k, w_v, w_g, state, log_gammas):
    rows, d_model = x2d.shape
    nseq, heads = state.shape[:2]
    anyspec = pl.BlockSpec(memory_space=pl.ANY)
    vspec = pl.BlockSpec(memory_space=pltpu.VMEM)
    return pl.pallas_call(
        mix_kernel,
        out_shape=(jax.ShapeDtypeStruct((rows, heads * 512), BF), jax.ShapeDtypeStruct(state.shape, F32)),
        in_specs=[pl.BlockSpec(memory_space=pltpu.SMEM), anyspec, vspec, vspec, vspec, vspec] + [anyspec] * 5,
        out_specs=(anyspec, anyspec),
        scratch_shapes=[
            pltpu.VMEM((rows, d_model), BF), pltpu.VMEM((rows, d_model), BF),
            pltpu.VMEM((6, d_model, 256), BF),
            pltpu.VMEM((2, nseq, 256, 512), F32), pltpu.VMEM((2, nseq, 256, 512), F32),
            pltpu.VMEM((rows, 256), BF), pltpu.VMEM((rows, 256), BF), pltpu.VMEM((rows, 512), BF),
            pltpu.VMEM((rows, 512), F32), pltpu.VMEM((2, rows, 512), BF),
            pltpu.SemaphoreType.DMA, pltpu.SemaphoreType.DMA((6,)), pltpu.SemaphoreType.DMA((2,)),
            pltpu.SemaphoreType.DMA((2,)), pltpu.SemaphoreType.DMA((2,)),
        ],
        compiler_params=pltpu.CompilerParams(vmem_limit_bytes=60 * 1024 * 1024),
        cost_estimate=pl.CostEstimate(flops=21_000_000_000, bytes_accessed=102_000_000, transcendentals=0),
        name='mix',
    )(log_gammas, x2d, cos_t, sin_t, gain, bias, w_q, w_k, w_v, w_g, state)


TN = 512


def ffn_kernel(z_hbm, x_hbm, g_ref, b_ref, wo, wup, wdn, o_hbm,
               zb, wa, wbb, ub, drv, xrv, h2, x1,
               zsem, x1sem, wosem, wupsem, wdnsem, ds_sem, dr_sem, xs_sem, xr_sem, hs_sem, hr_sem, ol_sem, os_sem, or_sem):
    tp = lax.axis_index('tp')
    core = lax.rem(tp, 2)
    sib = {'tp': tp + 1 - 2 * core}
    nbr = {'tp': lax.rem(tp + 2, 4)}
    nt = wo.shape[1] // TN
    ku = wup.shape[1] // 256
    hrows = ub.shape[2]

    def wo_copy(n):
        return pltpu.make_async_copy(wo.at[:, pl.ds(pl.multiple_of(n * TN, TN), TN)], wbb.at[n], wosem.at[n])

    def wdn_copy(n):
        return pltpu.make_async_copy(wdn.at[:, pl.ds(pl.multiple_of(n * TN, TN), TN)], wbb.at[n], wdnsem.at[n])

    def wup_copy(n):
        return pltpu.make_async_copy(wup.at[:, pl.ds(pl.multiple_of(n * 256, 256), 256)], wa.at[n], wupsem.at[n])

    def x1_copy(c):
        src = x_hbm.at[pl.ds(pl.multiple_of((c * 2 + core) * hrows, hrows), hrows)]
        return pltpu.make_async_copy(src, x1.at[c], x1sem.at[c])

    zcopy = pltpu.make_async_copy(z_hbm, zb, zsem)
    zcopy.start()

    def start_wo(n, carry):
        wo_copy(n).start()
        return carry
    lax.fori_loop(0, nt, start_wo, 0)
    x1_copy(0).start()
    x1_copy(1).start()

    def start_wup(n, carry):
        wup_copy(n).start()
        return carry
    lax.fori_loop(0, ku, start_wup, 0)

    barrier = pltpu.get_barrier_semaphore()
    pl.semaphore_signal(barrier, inc=1, device_id=sib, device_id_type=MESH)
    pl.semaphore_signal(barrier, inc=1, device_id=nbr, device_id_type=MESH)
    pl.semaphore_wait(barrier, 2)

    def d_copy(r, c, n):
        return pltpu.make_async_remote_copy(
            src_ref=ub.at[c * 2 + 1 - core, n], dst_ref=drv.at[c, n], send_sem=ds_sem.at[r, c, n], recv_sem=dr_sem.at[r, c, n],
            device_id=sib, device_id_type=MESH)

    def x_copy(r, c, n):
        return pltpu.make_async_remote_copy(
            src_ref=ub.at[c * 2 + core, n], dst_ref=xrv.at[r, c, n], send_sem=xs_sem.at[r, c, n], recv_sem=xr_sem.at[r, c, n],
            device_id=nbr, device_id_type=MESH)

    def forward(r, c, n):
        d_copy(r, c, n).wait_recv()
        own = ub[c * 2 + core, n].astype(F32)
        ub[c * 2 + core, n] = (own + drv[c, n].astype(F32)).astype(BF)
        x_copy(r, c, n).start()

    lag = 2
    zcopy.wait()

    def wo_step(n, carry):
        wo_copy(n).wait()
        res = dot(zb[...], wbb[n]).astype(BF)
        for j in range(4):
            ub[j, n] = res[j * hrows:(j + 1) * hrows]
        d_copy(0, 0, n).start()
        d_copy(0, 1, n).start()
        wdn_copy(n).start()

        @pl.when(n >= lag)
        def _():
            forward(0, 0, n - lag)
        return carry
    lax.fori_loop(0, nt, wo_step, 0)
    for n in range(nt - lag, nt):
        forward(0, 0, n)

    def fwd1(n, carry):
        forward(0, 1, n)
        return carry
    lax.fori_loop(0, nt, fwd1, 0)

    def h_copy(c):
        own = h2.at[c, pl.ds(pl.multiple_of(core * hrows, hrows), hrows)]
        return pltpu.make_async_remote_copy(src_ref=own, dst_ref=own, send_sem=hs_sem.at[c], recv_sem=hr_sem.at[c],
                                            device_id=sib, device_id_type=MESH)

    def chunk(c):
        x1_copy(c).wait()
        for n in range(nt):
            x_copy(0, c, n).wait_recv()

        def ln_rows(r, carry):
            rows = pl.ds(pl.multiple_of(r * 16, 16), 16)
            total = jnp.concatenate(
                [(ub[c * 2 + core, n, rows, :].astype(F32) + xrv[0, c, n, rows, :].astype(F32)).astype(BF) for n in range(nt)], axis=-1)
            mid = (x1[c, rows, :].astype(F32) + total.astype(F32)).astype(BF)
            x1[c, rows, :] = mid
            hrow = pl.ds(pl.multiple_of(core * hrows + r * 16, 16), 16)
            h2[c, hrow, :] = layer_norm(mid.astype(F32), g_ref[...], b_ref[...]).astype(BF)
            return carry
        lax.fori_loop(0, hrows // 16, ln_rows, 0)
        h_copy(c).start()

        def drain(n, carry):
            d_copy(0, c, n).wait_send()
            x_copy(0, c, n).wait_send()
            return carry
        lax.fori_loop(0, nt, drain, 0)
        h_copy(c).wait_recv()

        def up_step(n, carry):
            if c == 0:
                wup_copy(n).wait()
            res = dot(h2[c], wa[n])
            res = 0.5 * res * (1.0 + lax.erf(res * (0.5 ** 0.5)))
            zb[c * 2 * hrows:(c + 1) * 2 * hrows, pl.ds(pl.multiple_of(n * 256, 256), 256)] = res.astype(BF)
            return carry
        lax.fori_loop(0, ku, up_step, 0)

        def down_step(n, carry):
            if c == 0:
                wdn_copy(n).wait()
            res = dot(zb[c * 2 * hrows:(c + 1) * 2 * hrows, :], wbb[n]).astype(BF)
            for j in range(2):
                ub[c * 2 + j, n] = res[j * hrows:(j + 1) * hrows]
            d_copy(1, c, n).start()

            @pl.when(n >= lag)
            def _():
                forward(1, c, n - lag)
            return carry
        lax.fori_loop(0, nt, down_step, 0)
        for n in range(nt - lag, nt):
            forward(1, c, n)

    chunk(0)
    chunk(1)

    def o_copies(c, n):
        src = x1.at[c, :, pl.ds(pl.multiple_of(n * TN, TN), TN)]
        dst = o_hbm.at[pl.ds(pl.multiple_of((c * 2 + core) * hrows, hrows), hrows), pl.ds(pl.multiple_of(n * TN, TN), TN)]
        local = pltpu.make_async_copy(src, dst, ol_sem.at[c, n])
        remote = pltpu.make_async_remote_copy(src_ref=src, dst_ref=dst, send_sem=os_sem.at[c, n], recv_sem=or_sem.at[c, n],
                                              device_id=sib, device_id_type=MESH)
        return local, remote

    for c in range(2):
        def out_step(n, carry):
            x_copy(1, c, n).wait_recv()
            cols = pl.ds(pl.multiple_of(n * TN, TN), TN)
            total = (ub[c * 2 + core, n].astype(F32) + xrv[1, c, n].astype(F32)).astype(BF)
            x1[c, :, cols] = (x1[c, :, cols].astype(F32) + total.astype(F32)).astype(BF)
            local, remote = o_copies(c, n)
            remote.start()
            local.start()
            return carry
        lax.fori_loop(0, nt, out_step, 0)
    for c in range(2):
        h_copy(c).wait_send()

        def fin(n, carry):
            d_copy(1, c, n).wait_send()
            x_copy(1, c, n).wait_send()
            local, remote = o_copies(c, n)
            local.wait()
            remote.wait_send()
            remote.wait_recv()
            return carry
        lax.fori_loop(0, nt, fin, 0)


def ffn_call(z2d, x2d, gain, bias, w_o, w_up, w_down):
    rows, d_model = x2d.shape
    width = z2d.shape[1]
    fdim = w_up.shape[1]
    nt = d_model // TN
    ku = fdim // 256
    hr = rows // 4
    anyspec = pl.BlockSpec(memory_space=pl.ANY)
    vspec = pl.BlockSpec(memory_space=pltpu.VMEM)
    dma = pltpu.SemaphoreType.DMA
    return pl.pallas_call(
        ffn_kernel,
        out_shape=jax.ShapeDtypeStruct((rows, d_model), BF),
        in_specs=[anyspec, anyspec, vspec, vspec, anyspec, anyspec, anyspec],
        out_specs=anyspec,
        scratch_shapes=[
            pltpu.VMEM((rows, width), BF),
            pltpu.VMEM((ku, d_model, 256), BF),
            pltpu.VMEM((nt, width, TN), BF),
            pltpu.VMEM((4, nt, hr, TN), BF),
            pltpu.VMEM((2, nt, hr, TN), BF),
            pltpu.VMEM((2, 2, nt, hr, TN), BF),
            pltpu.VMEM((2, 2 * hr, d_model), BF),
            pltpu.VMEM((2, hr, d_model), BF),
            dma, dma((2,)), dma((nt,)), dma((ku,)), dma((nt,)),
            dma((2, 2, nt)), dma((2, 2, nt)), dma((2, 2, nt)), dma((2, 2, nt)), dma((2,)), dma((2,)),
            dma((2, nt)), dma((2, nt)), dma((2, nt)),
        ],
        compiler_params=pltpu.CompilerParams(collective_id=0, has_side_effects=True, vmem_limit_bytes=67043328),
        cost_estimate=pl.CostEstimate(flops=20_000_000_000, bytes_accessed=85_000_000, transcendentals=0),
        name='ffn',
    )(z2d, x2d, gain, bias, w_o, w_up, w_down)


def solution(mesh):
    def local_layer(x_in, start_pos, kv_state, ln1_gain, ln1_bias, w_q, w_k, w_v, w_g, w_o, ln2_gain, ln2_bias, w_up, w_down):
        nseq, clen, d_model = x_in.shape
        x2d = x_in.reshape(nseq * clen, d_model)
        cos_t, sin_t = rope_tables(start_pos, clen, kv_state.shape[2])
        num_heads = kv_state.shape[1] * mesh.shape['tp']
        log_gammas = jnp.asarray(np.log1p(-np.exp2(-5.0 - np.arange(num_heads))).astype(np.float32))
        z2d, new_state = mix_call(x2d, cos_t, sin_t, ln1_gain.reshape(1, -1), ln1_bias.reshape(1, -1),
                                  w_q, w_k, w_v, w_g, kv_state, log_gammas)
        out = ffn_call(z2d, x2d, ln2_gain.reshape(1, -1), ln2_bias.reshape(1, -1), w_o, w_up, w_down)
        return out.reshape(x_in.shape), new_state

    in_specs = (P('dp', None, None), P('dp'), P('dp', 'tp', None, None), P(), P(), P(None, 'tp'), P(None, 'tp'), P(None, 'tp'), P(None, 'tp'), P('tp', None), P(), P(), P(None, 'tp'), P('tp', None))
    out_specs = (P('dp', None, None), P('dp', 'tp', None, None))
    return jax.shard_map(local_layer, mesh=mesh, in_specs=in_specs, out_specs=out_specs, check_vma=False)
```

time: 357 us -> 143 us (0.40)
  Pallas kernels: 0 us -> 136 us
  matrix products: 113 us -> 0 us
  waiting for transfers between devices: 104 us -> 0 us
  local copies, waits for them, and re-layouts: 107 us -> 3.48 us
  between operations: 14.2 us -> 0.65 us
  other arithmetic: 15.5 us -> 1.96 us
    pallas_call x0 -> x2, Pallas kernels: none -> 136 us  [the longest x1 68.9 us: ffn_call(): pl.pallas_call(ffn_kernel, out_shape=jax.ShapeDtypeStruct((rows, d_model)...]
    dot_general x10 -> x0, matrix products: 113 us -> none  [the longest x1 17.6 us: feed_forward(): jnp.einsum('bcf,fd->bcd', activated, w_down, preferred_element_type=jnp.f...]
    psum x2 -> x0, waiting for transfers between devices: 104 us -> none  [the longest x1 58.9 us: local_layer(): attn_out = lax.psum(attn_part, 'tp')]
    unnamed x22 -> x1, local copies, waits for them, and re-layouts: 107 us -> 3.4 us
    reduce_sum x5 -> x0, other arithmetic: 7.29 us -> none  [the longest x2 5.1 us: layer_norm(): row_mean = jnp.mean(x_f32, axis=-1, keepdims=True)]
  transfers between devices with their start and end apart: 2 -> 0, of which waited for: 2 -> 0; matrix products, arithmetic and copies ran while one was open for 3% -> 0% of each run, Pallas kernels for 0% -> 0%
where the time goes in v1:
time: 143 us
  Pallas kernels  136 us (95%)
  local copies, waits for them, and re-layouts  3.48 us (2%)
  other arithmetic  1.96 us (1%)
    pallas_call x1, Pallas kernels, ffn_call(): pl.pallas_call(ffn_kernel, out_shape=jax.ShapeDtypeStruct((rows, d_model)...  68.9 us
    pallas_call x1, Pallas kernels, mix_call(): pl.pallas_call(mix_kernel, out_shape=(jax.ShapeDtypeStruct((rows, heads *...  67.6 us
    unnamed x1, local copies, waits for them, and re-layouts  3.4 us

profile of v1, /device:TPU:0, one launch (start us, length us, event | category | flops | bytes accessed | tf_op | source)
XLA Modules:
  0.0 142.6 jit_solution(10674460611033576144)
XLA Ops:
  0.6 0.7 add_convert_fusion
  1.4 0.1 convert_element_type.18
  1.5 1.2 multiply_sine_fusion
  2.7 67.6 %mix.1 = (bf16[256,2560]{1,0:T(8,128)(2,1)}, f32[4,5,256,512]{3,2,1,0:T(8,128)}) custom-call(f32[20]{0:T(128)} %constant.7.clone.lg_ref, bf16[256,5120]{1,0:T(8,128)(2,1)} %bitcast.6, f32[256,128]{1,0:T(8,128)} %get-tuple-element.7.cos_ref, f32[256,128]{1,0:T(8,128)} %get-tuple-element.6.sin_ref, f32[1,5120]{1,0:T(1,128)} %bitcast.9, f32[1,5120]{1,0:T(1,128)} %bitcast.10, ...), custom_call_target="tpu_custom_call" | custom-call | flops 20999999488 | bytes 102000000 | tf_op jit(solution)/shard_map/mix/pallas_call | solution.py:163
  70.2 68.9 %ffn.1 = bf16[256,5120]{1,0:T(8,128)(2,1)} custom-call(bf16[256,2560]{1,0:T(8,128)(2,1)} %get-tuple-element.4.z_hbm, bf16[256,5120]{1,0:T(8,128)(2,1)} %bitcast.7, f32[1,5120]{1,0:T(1,128)} %bitcast.11, f32[1,5120]{1,0:T(1,128)} %bitcast.12, bf16[2560,5120]{1,0:T(8,128)(2,1)} %wo.1, bf16[5120,2560]{1,0:T(8,128)(2,1)} %wup.1, bf16[2560,5120]{1,0:T(8,128)(2,1)} %wdn.1), custom_call_target="tpu_custom_call" | custom-call | flops 20000000000 | bytes 85000000 | tf_op jit(solution)/shard_map/ffn/pallas_call | solution.py:371
  139.2 3.4 %copy.18 = bf16[4,64,5120]{2,1,0:T(8,128)(2,1)} copy(bf16[4,64,5120]{2,1,0:T(8,128)(2,1)} %bitcast.8) | data formatting | bytes 5242880
  (1 shorter events, 0.0 us)

commit v2 on v1

--- a/solution.py
+++ b/solution.py
@@ -38,8 +38,24 @@
     return jnp.dot(lhs, rhs, preferred_element_type=F32)
 
 
+def ln_rows(load, store, g_ref, b_ref, width):
+    cols = [slice(c, c + 256) for c in range(0, width, 256)]
+    total = load(cols[0])
+    for col in cols[1:]:
+        total = total + load(col)
+    mean = jnp.sum(total, axis=-1, keepdims=True) * (1.0 / width)
+    total = None
+    for col in cols:
+        cent = load(col) - mean
+        total = cent * cent if total is None else total + cent * cent
+    var = jnp.sum(total, axis=-1, keepdims=True) * (1.0 / width)
+    scale = lax.rsqrt(var + NORM_EPS)
+    for col in cols:
+        store(col, ((load(col) - mean) * scale * g_ref[:, col] + b_ref[:, col]).astype(BF))
+
+
 def mix_kernel(lg_ref, x_hbm, cos_ref, sin_ref, g_ref, b_ref, wq, wk, wv, wg, s_hbm, z_hbm, so_hbm,
-               xb, hb, wb, sb, sob, qb, kb, vb, gb, zb, xsem, wsem, ssem, sosem, zsem):
+               xb, hb, wb, sb, sob, qb, kb, vb, gb, scb, sth, stl, kdb, ob, zb, xsem, wsem, ssem, sosem, zsem):
     heads = wq.shape[1] // 256
     nseq = s_hbm.shape[0]
     clen = x_hbm.shape[0] // nseq
@@ -68,20 +84,26 @@
         slot = lax.rem(head, 2)
         return pltpu.make_async_copy(zb.at[slot], z_hbm.at[:, pl.ds(pl.multiple_of(head * 512, 512), 512)], zsem.at[slot])
 
-    xcopy = pltpu.make_async_copy(x_hbm, xb, xsem)
-    xcopy.start()
-    for i in range(3):
+    def xcopy(s):
+        rows = pl.ds(pl.multiple_of(s * clen, clen), clen)
+        return pltpu.make_async_copy(x_hbm.at[rows], xb.at[rows], xsem.at[s])
+
+    for s in range(nseq):
+        xcopy(s).start()
+    for i in range(6):
         wcopy(0, i).start()
     scopy(0).start()
-    for i in range(3, 6):
-        wcopy(0, i).start()
-    xcopy.wait()
-
-    def ln_rows(r, carry):
-        rows = pl.ds(pl.multiple_of(r * 16, 16), 16)
-        hb[rows, :] = layer_norm(xb[rows, :].astype(F32), g_ref[...], b_ref[...]).astype(BF)
-        return carry
-    lax.fori_loop(0, xb.shape[0] // 16, ln_rows, 0)
+    scopy(1).start()
+
+    def ln_body(s, carry):
+        xcopy(s).wait()
+        rows = pl.ds(pl.multiple_of(s * clen, clen), clen)
+
+        def store(col, val):
+            hb[rows, col] = val
+        ln_rows(lambda col: xb[rows, col].astype(F32), store, g_ref, b_ref, xb.shape[1])
+        return carry
+    lax.fori_loop(0, nseq, ln_body, 0)
 
     step_i = lax.broadcasted_iota(jnp.int32, (clen, clen), 0)
     step_j = lax.broadcasted_iota(jnp.int32, (clen, clen), 1)
@@ -89,68 +111,127 @@
     tok_q = lax.broadcasted_iota(jnp.int32, (clen, 512), 0).astype(F32)
     tok_k = lax.broadcasted_iota(jnp.int32, (clen, 256), 0).astype(F32)
 
+    def proj2(head, i):
+        return dot(hb[...], wb[i]), dot(hb[...], wb[i + 1])
+
+    def wait2(head, i):
+        wcopy(head, i).wait()
+        wcopy(head, i + 1).wait()
+
+    def next2(head, i):
+        @pl.when(head + 1 < heads)
+        def _():
+            wcopy(head + 1, i).start()
+            wcopy(head + 1, i + 1).start()
+
+    def proj_qk(head, slot):
+        cos_t = cos_ref[...]
+        sin_t = sin_ref[...]
+        q, k = proj2(head, 0)
+        qb[slot, :, :128] = (q[:, :128] * cos_t - q[:, 128:] * sin_t).astype(BF)
+        qb[slot, :, 128:] = (q[:, 128:] * cos_t + q[:, :128] * sin_t).astype(BF)
+        kb[slot, :, :128] = ((k[:, :128] * cos_t - k[:, 128:] * sin_t) * 0.0625).astype(BF)
+        kb[slot, :, 128:] = ((k[:, 128:] * cos_t + k[:, :128] * sin_t) * 0.0625).astype(BF)
+
+    def proj_v(head, slot):
+        for half, val in enumerate(proj2(head, 2)):
+            val = val.astype(BF)
+            for s in range(nseq):
+                for copy in range(2):
+                    vb[slot, s, copy * clen:(copy + 1) * clen, half * 256:(half + 1) * 256] = val[s * clen:(s + 1) * clen]
+
+    def proj_g(head, slot):
+        gb[slot, :, :256], gb[slot, :, 256:] = proj2(head, 4)
+
+    def seq_rows(s):
+        return slice(s * clen, (s + 1) * clen)
+
+    def ret_scores(slot):
+        return [lax.dot_general(qb[slot, seq_rows(s), :], kb[slot, seq_rows(s), :], (((1,), (1,)), ((), ())),
+                                preferred_element_type=F32) for s in range(nseq)]
+
+    def ret_prepare(head, slot, scores):
+        log_g = lg_ref[first_head + head]
+        inner_decay = jnp.where(gap >= 0, jnp.exp(jnp.maximum(gap, 0).astype(F32) * log_g), 0.0)
+        key_decay = jnp.exp((clen - 1.0 - tok_k) * log_g)
+        for s in range(nseq):
+            sth[s], stl[s] = split2(sb[slot, s])
+            kdb[s, :clen], kdb[s, clen:] = split2(kb[slot, seq_rows(s), :].astype(F32) * key_decay)
+            high, low = split2(scores[s] * inner_decay)
+            scb[s] = jnp.concatenate([high, low], axis=-1)
+
+    def ret_out(head, slot):
+        log_g = lg_ref[first_head + head]
+        query_decay = jnp.exp((tok_q + 1.0) * log_g)
+        state_decay = jnp.exp(jnp.full((1, 512), clen, F32) * log_g)
+        for s in range(nseq):
+            q = qb[slot, seq_rows(s), :]
+            ob[seq_rows(s), :] = dot(scb[s], vb[slot, s]) + (dot(q, sth[s]) + dot(q, stl[s])) * query_decay
+            update = lax.dot_general(kdb[s], vb[slot, s], (((0,), (0,)), ((), ())), preferred_element_type=F32)
+            sob[slot, s] = sb[slot, s] * state_decay + update
+
+    def ret_gate(slot):
+        for s in range(nseq):
+            out = ob[seq_rows(s), :]
+            mean = jnp.mean(out, axis=-1, keepdims=True)
+            cent = out - mean
+            var = jnp.mean(cent * cent, axis=-1, keepdims=True)
+            gates = gb[slot, seq_rows(s), :]
+            zb[slot, seq_rows(s), :] = (gates * jax.nn.sigmoid(gates) * (cent * lax.rsqrt(var + GROUP_EPS))).astype(BF)
+
+    wait2(0, 0)
+    proj_qk(0, 0)
+    next2(0, 0)
+    wait2(0, 2)
+    proj_v(0, 0)
+    next2(0, 2)
+    wait2(0, 4)
+    proj_g(0, 0)
+    next2(0, 4)
+
     def head_body(head, carry):
-        def proj(i):
-            wcopy(head, i).wait()
-            res = dot(hb[...], wb[i])
-
-            @pl.when(head + 1 < heads)
-            def _():
-                wcopy(head + 1, i).start()
-            return res
+        prev = head - 1
+        slot = lax.rem(head, 2)
+        old = 1 - slot
+        scopy(prev).wait()
+
+        @pl.when(prev >= 2)
+        def _():
+            socopy(prev - 2).wait()
+            zcopy(prev - 2).wait()
+        wait2(head, 0)
+        scores = ret_scores(old)
+        proj_qk(head, slot)
+        ret_prepare(prev, old, scores)
+        next2(head, 0)
+        wait2(head, 2)
+        ret_out(prev, old)
+        proj_v(head, slot)
+        next2(head, 2)
+        socopy(prev).start()
 
         @pl.when(head + 1 < heads)
         def _():
             scopy(head + 1).start()
-
-        cos_t = cos_ref[...]
-        sin_t = sin_ref[...]
-        res = proj(0)
-        qb[:, :128] = (res[:, :128] * cos_t - res[:, 128:] * sin_t).astype(BF)
-        qb[:, 128:] = (res[:, 128:] * cos_t + res[:, :128] * sin_t).astype(BF)
-        res = proj(1)
-        kb[:, :128] = ((res[:, :128] * cos_t - res[:, 128:] * sin_t) * 0.0625).astype(BF)
-        kb[:, 128:] = ((res[:, 128:] * cos_t + res[:, :128] * sin_t) * 0.0625).astype(BF)
-        vb[:, :256] = proj(2).astype(BF)
-        vb[:, 256:] = proj(3).astype(BF)
-        gb[:, :256] = proj(4)
-        gb[:, 256:] = proj(5)
-
-        log_g = lg_ref[first_head + head]
-        inner_decay = jnp.where(gap >= 0, jnp.exp(jnp.maximum(gap, 0).astype(F32) * log_g), 0.0)
-        query_decay = jnp.exp((tok_q + 1.0) * log_g)
-        key_decay = jnp.exp((clen - 1.0 - tok_k) * log_g)
-        state_decay = jnp.exp(jnp.full((1, 512), clen, F32) * log_g)
-        slot = lax.rem(head, 2)
-        scopy(head).wait()
-
-        @pl.when(head >= 2)
-        def _():
-            socopy(head - 2).wait()
-            zcopy(head - 2).wait()
-
-        for s in range(nseq):
-            rows = slice(s * clen, (s + 1) * clen)
-            q, k, v = qb[rows, :], kb[rows, :], vb[rows, :]
-            scores = lax.dot_general(q, k, (((1,), (1,)), ((), ())), preferred_element_type=F32) * inner_decay
-            sc_hi, sc_lo = split2(scores)
-            state = sb[slot, s]
-            st_hi, st_lo = split2(state)
-            out = dot(sc_hi, v) + dot(sc_lo, v) + (dot(q, st_hi) + dot(q, st_lo)) * query_decay
-            mean = jnp.mean(out, axis=-1, keepdims=True)
-            cent = out - mean
-            var = jnp.mean(cent * cent, axis=-1, keepdims=True)
-            gates = gb[rows, :]
-            zb[slot, rows, :] = (gates * jax.nn.sigmoid(gates) * (cent * lax.rsqrt(var + GROUP_EPS))).astype(BF)
-            kd_hi, kd_lo = split2(k.astype(F32) * key_decay)
-            tdot = lambda a: lax.dot_general(a, v, (((0,), (0,)), ((), ())), preferred_element_type=F32)
-            sob[slot, s] = state * state_decay + (tdot(kd_hi) + tdot(kd_lo))
-        socopy(head).start()
-        zcopy(head).start()
-        return carry
-
-    lax.fori_loop(0, heads, head_body, 0)
-    for head in (heads - 2, heads - 1):
+        wait2(head, 4)
+        proj_g(head, slot)
+        ret_gate(old)
+        next2(head, 4)
+        zcopy(prev).start()
+        return carry
+
+    lax.fori_loop(1, heads, head_body, 0)
+    last = heads - 1
+    slot = last % 2
+    scopy(last).wait()
+    socopy(last - 2).wait()
+    zcopy(last - 2).wait()
+    ret_prepare(last, slot, ret_scores(slot))
+    ret_out(last, slot)
+    socopy(last).start()
+    ret_gate(slot)
+    zcopy(last).start()
+    for head in (last - 1, last):
         socopy(head).wait()
         zcopy(head).wait()
 
@@ -158,6 +239,7 @@
 def mix_call(x2d, cos_t, sin_t, gain, bias, w_q, w_k, w_v, w_g, state, log_gammas):
     rows, d_model = x2d.shape
     nseq, heads = state.shape[:2]
+    clen = rows // nseq
     anyspec = pl.BlockSpec(memory_space=pl.ANY)
     vspec = pl.BlockSpec(memory_space=pltpu.VMEM)
     return pl.pallas_call(
@@ -169,9 +251,11 @@
             pltpu.VMEM((rows, d_model), BF), pltpu.VMEM((rows, d_model), BF),
             pltpu.VMEM((6, d_model, 256), BF),
             pltpu.VMEM((2, nseq, 256, 512), F32), pltpu.VMEM((2, nseq, 256, 512), F32),
-            pltpu.VMEM((rows, 256), BF), pltpu.VMEM((rows, 256), BF), pltpu.VMEM((rows, 512), BF),
-            pltpu.VMEM((rows, 512), F32), pltpu.VMEM((2, rows, 512), BF),
-            pltpu.SemaphoreType.DMA, pltpu.SemaphoreType.DMA((6,)), pltpu.SemaphoreType.DMA((2,)),
+            pltpu.VMEM((2, rows, 256), BF), pltpu.VMEM((2, rows, 256), BF), pltpu.VMEM((2, nseq, 2 * clen, 512), BF),
+            pltpu.VMEM((2, rows, 512), F32),
+            pltpu.VMEM((nseq, clen, 2 * clen), BF), pltpu.VMEM((nseq, 256, 512), BF), pltpu.VMEM((nseq, 256, 512), BF),
+            pltpu.VMEM((nseq, 2 * clen, 256), BF), pltpu.VMEM((rows, 512), F32), pltpu.VMEM((2, rows, 512), BF),
+            pltpu.SemaphoreType.DMA((nseq,)), pltpu.SemaphoreType.DMA((6,)), pltpu.SemaphoreType.DMA((2,)),
             pltpu.SemaphoreType.DMA((2,)), pltpu.SemaphoreType.DMA((2,)),
         ],
         compiler_params=pltpu.CompilerParams(vmem_limit_bytes=60 * 1024 * 1024),

time: 143 us -> 114 us (0.80)
  Pallas kernels: 136 us -> 108 us
    pallas_call x1, Pallas kernels: 67.6 us -> 38.9 us  [mix_call(): pl.pallas_call(mix_kernel, out_shape=(jax.ShapeDtypeStruct((rows, heads *...]
where the time goes in v2:
time: 114 us
  Pallas kernels  108 us (95%)
  local copies, waits for them, and re-layouts  3.48 us (3%)
  other arithmetic  1.96 us (2%)
    pallas_call x1, Pallas kernels, ffn_call(): pl.pallas_call(ffn_kernel, out_shape=jax.ShapeDtypeStruct((rows, d_model)...  68.9 us
    pallas_call x1, Pallas kernels, mix_call(): pl.pallas_call(mix_kernel, out_shape=(jax.ShapeDtypeStruct((rows, heads *...  38.9 us
    unnamed x1, local copies, waits for them, and re-layouts  3.4 us

profile of v2, /device:TPU:0, one launch (start us, length us, event | category | flops | bytes accessed | tf_op | source)
XLA Modules:
  0.0 113.9 jit_solution(6952615893477995165)
XLA Ops:
  0.6 0.7 add_convert_fusion
  1.4 0.1 convert_element_type.18
  1.5 1.2 %multiply_sine_fusion = (f32[256,128]{1,0:T(8,128)}, f32[256,128]{1,0:T(8,128)}) fusion(f32[128]{0:T(128)S(1)} %multiply_power_fusion, f32[256]{0:T(256)S(1)} %convert_element_type.18), kind=kLoop, calls=%fused_computation | loop fusion | flops 32768 | bytes 263680 | tf_op jit(solution)/shard_map/sin | solution.py:29
  2.7 38.9 %mix.1 = (bf16[256,2560]{1,0:T(8,128)(2,1)}, f32[4,5,256,512]{3,2,1,0:T(8,128)}) custom-call(f32[20]{0:T(128)} %constant.7.clone.lg_ref, bf16[256,5120]{1,0:T(8,128)(2,1)} %bitcast.6, f32[256,128]{1,0:T(8,128)} %get-tuple-element.7.cos_ref, f32[256,128]{1,0:T(8,128)} %get-tuple-element.6.sin_ref, f32[1,5120]{1,0:T(1,128)} %bitcast.9, f32[1,5120]{1,0:T(1,128)} %bitcast.10, ...), custom_call_target="tpu_custom_call" | custom-call | flops 20999999488 | bytes 102000000 | tf_op jit(solution)/shard_map/mix/pallas_call | solution.py:245
  41.6 68.9 %ffn.1 = bf16[256,5120]{1,0:T(8,128)(2,1)} custom-call(bf16[256,2560]{1,0:T(8,128)(2,1)} %get-tuple-element.4.z_hbm, bf16[256,5120]{1,0:T(8,128)(2,1)} %bitcast.7, f32[1,5120]{1,0:T(1,128)} %bitcast.11, f32[1,5120]{1,0:T(1,128)} %bitcast.12, bf16[2560,5120]{1,0:T(8,128)(2,1)} %wo.1, bf16[5120,2560]{1,0:T(8,128)(2,1)} %wup.1, bf16[2560,5120]{1,0:T(8,128)(2,1)} %wdn.1), custom_call_target="tpu_custom_call" | custom-call | flops 20000000000 | bytes 85000000 | tf_op jit(solution)/shard_map/ffn/pallas_call | solution.py:455
  110.5 3.4 %copy.18 = bf16[4,64,5120]{2,1,0:T(8,128)(2,1)} copy(bf16[4,64,5120]{2,1,0:T(8,128)(2,1)} %bitcast.8) | data formatting | bytes 5242880
  (1 shorter events, 0.0 us)

commit v3 on v2

--- a/solution.py
+++ b/solution.py
@@ -12,6 +12,7 @@
 BF = jnp.bfloat16
 F32 = jnp.float32
 MESH = pl.DeviceIdType.MESH
+SLOTS = 4
 
 
 def layer_norm(x_f32, norm_gain, norm_bias):
@@ -21,12 +22,11 @@
     return centered * lax.rsqrt(variance + NORM_EPS) * norm_gain + norm_bias
 
 
-def rope_tables(first_pos, chunk_len, key_dim):
+def rope_constants(chunk_len, key_dim):
     half_dim = key_dim // 2
-    inv_freq = jnp.power(ROPE_BASE, -jnp.arange(half_dim).astype(F32) / half_dim)
-    positions = (first_pos[:, None] + jnp.arange(chunk_len)[None, :]).astype(F32)
-    angles = (positions[:, :, None] * inv_freq).reshape(-1, half_dim)
-    return jnp.cos(angles), jnp.sin(angles)
+    inv_freq = np.power(ROPE_BASE, -np.arange(half_dim) / half_dim).astype(np.float32)
+    step_angles = np.arange(chunk_len)[:, None] * inv_freq.astype(np.float64)[None, :]
+    return jnp.asarray(inv_freq[None, :]), jnp.asarray(np.cos(step_angles).astype(np.float32)), jnp.asarray(np.sin(step_angles).astype(np.float32))
 
 
 def split2(val):
@@ -54,23 +54,25 @@
         store(col, ((load(col) - mean) * scale * g_ref[:, col] + b_ref[:, col]).astype(BF))
 
 
-def mix_kernel(lg_ref, x_hbm, cos_ref, sin_ref, g_ref, b_ref, wq, wk, wv, wg, s_hbm, z_hbm, so_hbm,
-               xb, hb, wb, sb, sob, qb, kb, vb, gb, scb, sth, stl, kdb, ob, zb, xsem, wsem, ssem, sosem, zsem):
+def mix_kernel(lg_ref, pos_ref, x_hbm, freq_ref, stepc_ref, steps_ref, g_ref, b_ref, wq, wk, wv, wg, s_hbm, z_hbm, so_hbm,
+               cos_ref, sin_ref, xb, hb, wb, sb, sob, qb, kb, vb, gb, scb, sth, stl, kdb, ob, zb, xsem, wsem, ssem, sosem, zsem):
     heads = wq.shape[1] // 256
     nseq = s_hbm.shape[0]
     clen = x_hbm.shape[0] // nseq
     first_head = lax.axis_index('tp') * heads
 
-    def wcopy(head, i):
+    def wcopies(head, i):
+        slot = lax.rem(head * 3 + i, SLOTS)
+        wide = pl.ds(pl.multiple_of(head * 512, 512), 512)
+        narrow = pl.ds(pl.multiple_of(head * 256, 256), 256)
         if i == 0:
-            src = wq.at[:, pl.ds(pl.multiple_of(head * 256, 256), 256)]
-        elif i == 1:
-            src = wk.at[:, pl.ds(pl.multiple_of(head * 256, 256), 256)]
-        elif i < 4:
-            src = wv.at[:, pl.ds(pl.multiple_of(head * 512 + (i - 2) * 256, 256), 256)]
-        else:
-            src = wg.at[:, pl.ds(pl.multiple_of(head * 512 + (i - 4) * 256, 256), 256)]
-        return pltpu.make_async_copy(src, wb.at[i], wsem.at[i])
+            return (pltpu.make_async_copy(wq.at[:, narrow], wb.at[slot, :, :256], wsem.at[slot, 0]),
+                    pltpu.make_async_copy(wk.at[:, narrow], wb.at[slot, :, 256:], wsem.at[slot, 1]))
+        return (pltpu.make_async_copy((wv if i == 1 else wg).at[:, wide], wb.at[slot], wsem.at[slot, 0]),)
+
+    def wstart(head, i):
+        for copy in wcopies(head, i):
+            copy.start()
 
     def scopy(head):
         slot = lax.rem(head, 2)
@@ -90,19 +92,32 @@
 
     for s in range(nseq):
         xcopy(s).start()
-    for i in range(6):
-        wcopy(0, i).start()
-    scopy(0).start()
-    scopy(1).start()
+    wstart(0, 0)
 
     def ln_body(s, carry):
-        xcopy(s).wait()
+        @pl.when(s < nseq - 1)
+        def _():
+            xcopy(s).wait()
         rows = pl.ds(pl.multiple_of(s * clen, clen), clen)
 
         def store(col, val):
             hb[rows, col] = val
         ln_rows(lambda col: xb[rows, col].astype(F32), store, g_ref, b_ref, xb.shape[1])
         return carry
+    def rope_body(s, carry):
+        angle = pos_ref[s].astype(F32) * freq_ref[...]
+        base_c, base_s = jnp.cos(angle), jnp.sin(angle)
+        rows = pl.ds(pl.multiple_of(s * clen, clen), clen)
+        cos_ref[rows, :] = base_c * stepc_ref[...] - base_s * steps_ref[...]
+        sin_ref[rows, :] = base_s * stepc_ref[...] + base_c * steps_ref[...]
+        return carry
+    lax.fori_loop(0, nseq, rope_body, 0)
+
+    xcopy(nseq - 1).wait()
+    for i in range(1, SLOTS):
+        wstart(i // 3, i % 3)
+    scopy(0).start()
+    scopy(1).start()
     lax.fori_loop(0, nseq, ln_body, 0)
 
     step_i = lax.broadcasted_iota(jnp.int32, (clen, clen), 0)
@@ -111,37 +126,38 @@
     tok_q = lax.broadcasted_iota(jnp.int32, (clen, 512), 0).astype(F32)
     tok_k = lax.broadcasted_iota(jnp.int32, (clen, 256), 0).astype(F32)
 
-    def proj2(head, i):
-        return dot(hb[...], wb[i]), dot(hb[...], wb[i + 1])
-
-    def wait2(head, i):
-        wcopy(head, i).wait()
-        wcopy(head, i + 1).wait()
-
-    def next2(head, i):
-        @pl.when(head + 1 < heads)
+    def project(head, i):
+        return dot(hb[...], wb[lax.rem(head * 3 + i, SLOTS)])
+
+    def wwait(head, i):
+        for copy in wcopies(head, i):
+            copy.wait()
+
+    def wnext(head, i):
+        next_head, next_i = head + (i + SLOTS) // 3, (i + SLOTS) % 3
+
+        @pl.when(next_head < heads)
         def _():
-            wcopy(head + 1, i).start()
-            wcopy(head + 1, i + 1).start()
+            wstart(next_head, next_i)
 
     def proj_qk(head, slot):
         cos_t = cos_ref[...]
         sin_t = sin_ref[...]
-        q, k = proj2(head, 0)
+        qk = project(head, 0)
+        q, k = qk[:, :256], qk[:, 256:]
         qb[slot, :, :128] = (q[:, :128] * cos_t - q[:, 128:] * sin_t).astype(BF)
         qb[slot, :, 128:] = (q[:, 128:] * cos_t + q[:, :128] * sin_t).astype(BF)
         kb[slot, :, :128] = ((k[:, :128] * cos_t - k[:, 128:] * sin_t) * 0.0625).astype(BF)
         kb[slot, :, 128:] = ((k[:, 128:] * cos_t + k[:, :128] * sin_t) * 0.0625).astype(BF)
 
     def proj_v(head, slot):
-        for half, val in enumerate(proj2(head, 2)):
-            val = val.astype(BF)
-            for s in range(nseq):
-                for copy in range(2):
-                    vb[slot, s, copy * clen:(copy + 1) * clen, half * 256:(half + 1) * 256] = val[s * clen:(s + 1) * clen]
+        val = project(head, 1).astype(BF)
+        for s in range(nseq):
+            for copy in range(2):
+                vb[slot, s, copy * clen:(copy + 1) * clen, :] = val[s * clen:(s + 1) * clen]
 
     def proj_g(head, slot):
-        gb[slot, :, :256], gb[slot, :, 256:] = proj2(head, 4)
+        gb[slot] = project(head, 2)
 
     def seq_rows(s):
         return slice(s * clen, (s + 1) * clen)
@@ -179,15 +195,15 @@
             gates = gb[slot, seq_rows(s), :]
             zb[slot, seq_rows(s), :] = (gates * jax.nn.sigmoid(gates) * (cent * lax.rsqrt(var + GROUP_EPS))).astype(BF)
 
-    wait2(0, 0)
+    wwait(0, 0)
     proj_qk(0, 0)
-    next2(0, 0)
-    wait2(0, 2)
+    wnext(0, 0)
+    wwait(0, 1)
     proj_v(0, 0)
-    next2(0, 2)
-    wait2(0, 4)
+    wnext(0, 1)
+    wwait(0, 2)
     proj_g(0, 0)
-    next2(0, 4)
+    wnext(0, 2)
 
     def head_body(head, carry):
         prev = head - 1
@@ -199,24 +215,24 @@
         def _():
             socopy(prev - 2).wait()
             zcopy(prev - 2).wait()
-        wait2(head, 0)
+        wwait(head, 0)
         scores = ret_scores(old)
         proj_qk(head, slot)
         ret_prepare(prev, old, scores)
-        next2(head, 0)
-        wait2(head, 2)
+        wnext(head, 0)
+        wwait(head, 1)
         ret_out(prev, old)
         proj_v(head, slot)
-        next2(head, 2)
+        wnext(head, 1)
         socopy(prev).start()
 
         @pl.when(head + 1 < heads)
         def _():
             scopy(head + 1).start()
-        wait2(head, 4)
+        wwait(head, 2)
         proj_g(head, slot)
         ret_gate(old)
-        next2(head, 4)
+        wnext(head, 2)
         zcopy(prev).start()
         return carry
 
@@ -236,32 +252,34 @@
         zcopy(head).wait()
 
 
-def mix_call(x2d, cos_t, sin_t, gain, bias, w_q, w_k, w_v, w_g, state, log_gammas):
+def mix_call(x2d, start_pos, gain, bias, w_q, w_k, w_v, w_g, state, log_gammas):
     rows, d_model = x2d.shape
     nseq, heads = state.shape[:2]
     clen = rows // nseq
+    smem = pl.BlockSpec(memory_space=pltpu.SMEM)
     anyspec = pl.BlockSpec(memory_space=pl.ANY)
     vspec = pl.BlockSpec(memory_space=pltpu.VMEM)
     return pl.pallas_call(
         mix_kernel,
         out_shape=(jax.ShapeDtypeStruct((rows, heads * 512), BF), jax.ShapeDtypeStruct(state.shape, F32)),
-        in_specs=[pl.BlockSpec(memory_space=pltpu.SMEM), anyspec, vspec, vspec, vspec, vspec] + [anyspec] * 5,
+        in_specs=[smem, smem, anyspec] + [vspec] * 5 + [anyspec] * 5,
         out_specs=(anyspec, anyspec),
         scratch_shapes=[
+            pltpu.VMEM((rows, 128), F32), pltpu.VMEM((rows, 128), F32),
             pltpu.VMEM((rows, d_model), BF), pltpu.VMEM((rows, d_model), BF),
-            pltpu.VMEM((6, d_model, 256), BF),
+            pltpu.VMEM((SLOTS, d_model, 512), BF),
             pltpu.VMEM((2, nseq, 256, 512), F32), pltpu.VMEM((2, nseq, 256, 512), F32),
             pltpu.VMEM((2, rows, 256), BF), pltpu.VMEM((2, rows, 256), BF), pltpu.VMEM((2, nseq, 2 * clen, 512), BF),
             pltpu.VMEM((2, rows, 512), F32),
             pltpu.VMEM((nseq, clen, 2 * clen), BF), pltpu.VMEM((nseq, 256, 512), BF), pltpu.VMEM((nseq, 256, 512), BF),
             pltpu.VMEM((nseq, 2 * clen, 256), BF), pltpu.VMEM((rows, 512), F32), pltpu.VMEM((2, rows, 512), BF),
-            pltpu.SemaphoreType.DMA((nseq,)), pltpu.SemaphoreType.DMA((6,)), pltpu.SemaphoreType.DMA((2,)),
+            pltpu.SemaphoreType.DMA((nseq,)), pltpu.SemaphoreType.DMA((SLOTS, 2)), pltpu.SemaphoreType.DMA((2,)),
             pltpu.SemaphoreType.DMA((2,)), pltpu.SemaphoreType.DMA((2,)),
         ],
         compiler_params=pltpu.CompilerParams(vmem_limit_bytes=60 * 1024 * 1024),
         cost_estimate=pl.CostEstimate(flops=21_000_000_000, bytes_accessed=102_000_000, transcendentals=0),
         name='mix',
-    )(log_gammas, x2d, cos_t, sin_t, gain, bias, w_q, w_k, w_v, w_g, state)
+    )(log_gammas, start_pos, x2d, *rope_constants(clen, state.shape[2]), gain, bias, w_q, w_k, w_v, w_g, state)
 
 
 TN = 512
@@ -298,11 +316,11 @@
         wo_copy(n).start()
         return carry
     lax.fori_loop(0, nt, start_wo, 0)
-    x1_copy(0).start()
-    x1_copy(1).start()
+    x1_copy(0).start(priority=1)
+    x1_copy(1).start(priority=1)
 
     def start_wup(n, carry):
-        wup_copy(n).start()
+        wup_copy(n).start(priority=1)
         return carry
     lax.fori_loop(0, ku, start_wup, 0)
 
@@ -337,15 +355,14 @@
             ub[j, n] = res[j * hrows:(j + 1) * hrows]
         d_copy(0, 0, n).start()
         d_copy(0, 1, n).start()
-        wdn_copy(n).start()
-
-        @pl.when(n >= lag)
+        wdn_copy(n).start(priority=1)
+
+        @pl.when(n >= 1)
         def _():
-            forward(0, 0, n - lag)
+            forward(0, 0, n - 1)
         return carry
     lax.fori_loop(0, nt, wo_step, 0)
-    for n in range(nt - lag, nt):
-        forward(0, 0, n)
+    forward(0, 0, nt - 1)
 
     def fwd1(n, carry):
         forward(0, 1, n)
@@ -480,10 +497,9 @@
     def local_layer(x_in, start_pos, kv_state, ln1_gain, ln1_bias, w_q, w_k, w_v, w_g, w_o, ln2_gain, ln2_bias, w_up, w_down):
         nseq, clen, d_model = x_in.shape
         x2d = x_in.reshape(nseq * clen, d_model)
-        cos_t, sin_t = rope_tables(start_pos, clen, kv_state.shape[2])
         num_heads = kv_state.shape[1] * mesh.shape['tp']
         log_gammas = jnp.asarray(np.log1p(-np.exp2(-5.0 - np.arange(num_heads))).astype(np.float32))
-        z2d, new_state = mix_call(x2d, cos_t, sin_t, ln1_gain.reshape(1, -1), ln1_bias.reshape(1, -1),
+        z2d, new_state = mix_call(x2d, start_pos, ln1_gain.reshape(1, -1), ln1_bias.reshape(1, -1),
                                   w_q, w_k, w_v, w_g, kv_state, log_gammas)
         out = ffn_call(z2d, x2d, ln2_gain.reshape(1, -1), ln2_bias.reshape(1, -1), w_o, w_up, w_down)
         return out.reshape(x_in.shape), new_state

time: 114 us -> 109 us (0.956)
  Pallas kernels: 108 us -> 105 us
  other arithmetic: 1.96 us -> 0 us
    pallas_call x1, Pallas kernels: 38.9 us -> 36.6 us  [mix_call(): pl.pallas_call(mix_kernel, out_shape=(jax.ShapeDtypeStruct((rows, heads *...]
    sin x1 -> x0, other arithmetic: 1.23 us -> none  [rope_tables(): return (jnp.cos(angles), jnp.sin(angles))]
where the time goes in v3:
time: 109 us
  Pallas kernels  105 us (96%)
  local copies, waits for them, and re-layouts  3.4 us (3%)
    pallas_call x1, Pallas kernels, ffn_call(): pl.pallas_call(ffn_kernel, out_shape=jax.ShapeDtypeStruct((rows, d_model)...  68.5 us
    pallas_call x1, Pallas kernels, mix_call(): pl.pallas_call(mix_kernel, out_shape=(jax.ShapeDtypeStruct((rows, heads *...  36.6 us
    unnamed x1, local copies, waits for them, and re-layouts  3.4 us

profile of v3, /device:TPU:0, one launch (start us, length us, event | category | flops | bytes accessed | tf_op | source)
XLA Modules:
  0.0 109.1 jit_solution(17795730692860808258)
XLA Ops:
  0.6 36.6 %mix.1 = (bf16[256,2560]{1,0:T(8,128)(2,1)}, f32[4,5,256,512]{3,2,1,0:T(8,128)}) custom-call(f32[20]{0:T(128)} %constant.8.clone.lg_ref, s32[4]{0:T(128)} %pos_ref.1, bf16[256,5120]{1,0:T(8,128)(2,1)} %bitcast.6, f32[1,128]{1,0:T(1,128)} %constant.9.clone.freq_ref, f32[64,128]{1,0:T(8,128)} %constant.10.clone.stepc_ref, f32[64,128]{1,0:T(8,128)} %constant.11.clone.steps_ref, ...), custom_call_target="tpu_custom_call" | custom-call | flops 20999999488 | bytes 102000000 | tf_op jit(solution)/shard_map/mix/pallas_call | solution.py:262
  37.2 68.5 %ffn.1 = bf16[256,5120]{1,0:T(8,128)(2,1)} custom-call(bf16[256,2560]{1,0:T(8,128)(2,1)} %get-tuple-element.4.z_hbm, bf16[256,5120]{1,0:T(8,128)(2,1)} %bitcast.7, f32[1,5120]{1,0:T(1,128)} %bitcast.11, f32[1,5120]{1,0:T(1,128)} %bitcast.12, bf16[2560,5120]{1,0:T(8,128)(2,1)} %wo.1, bf16[5120,2560]{1,0:T(8,128)(2,1)} %wup.1, bf16[2560,5120]{1,0:T(8,128)(2,1)} %wdn.1), custom_call_target="tpu_custom_call" | custom-call | flops 20000000000 | bytes 85000000 | tf_op jit(solution)/shard_map/ffn/pallas_call | solution.py:472
  105.7 3.4 %copy.21 = bf16[4,64,5120]{2,1,0:T(8,128)(2,1)} copy(bf16[4,64,5120]{2,1,0:T(8,128)(2,1)} %bitcast.8) | data formatting | bytes 5242880

commit v4 on v3

--- a/solution.py
+++ b/solution.py
@@ -54,8 +54,8 @@
         store(col, ((load(col) - mean) * scale * g_ref[:, col] + b_ref[:, col]).astype(BF))
 
 
-def mix_kernel(lg_ref, pos_ref, x_hbm, freq_ref, stepc_ref, steps_ref, g_ref, b_ref, wq, wk, wv, wg, s_hbm, z_hbm, so_hbm,
-               cos_ref, sin_ref, xb, hb, wb, sb, sob, qb, kb, vb, gb, scb, sth, stl, kdb, ob, zb, xsem, wsem, ssem, sosem, zsem):
+def mix_kernel(lg_hbm, pos_hbm, x_hbm, freq_hbm, stepc_hbm, steps_hbm, g_hbm, b_hbm, wq, wk, wv, wg, s_hbm, z_hbm, so_hbm,
+               lg_ref, pos_ref, freq_ref, stepc_ref, steps_ref, g_ref, b_ref, small_sem, cos_ref, sin_ref, xb, hb, wb, sb, sob, qb, kb, vb, gb, scb, sth, stl, kdb, ob, zb, xsem, wsem, ssem, sosem, zsem):
     heads = wq.shape[1] // 256
     nseq = s_hbm.shape[0]
     clen = x_hbm.shape[0] // nseq
@@ -90,14 +90,26 @@
         rows = pl.ds(pl.multiple_of(s * clen, clen), clen)
         return pltpu.make_async_copy(x_hbm.at[rows], xb.at[rows], xsem.at[s])
 
+    small = ((pos_hbm, pos_ref), (freq_hbm, freq_ref), (stepc_hbm, stepc_ref), (steps_hbm, steps_ref),
+             (g_hbm, g_ref), (b_hbm, b_ref), (lg_hbm, lg_ref))
+    small = [pltpu.make_async_copy(src, dst, small_sem.at[i]) for i, (src, dst) in enumerate(small)]
+    for copy in small:
+        copy.start()
     for s in range(nseq):
         xcopy(s).start()
     wstart(0, 0)
+    for copy in small:
+        copy.wait()
 
     def ln_body(s, carry):
-        @pl.when(s < nseq - 1)
+        xcopy(s).wait()
+
+        @pl.when(s == nseq - 1)
         def _():
-            xcopy(s).wait()
+            for i in range(1, SLOTS):
+                wstart(i // 3, i % 3)
+            scopy(0).start()
+            scopy(1).start()
         rows = pl.ds(pl.multiple_of(s * clen, clen), clen)
 
         def store(col, val):
@@ -113,11 +125,6 @@
         return carry
     lax.fori_loop(0, nseq, rope_body, 0)
 
-    xcopy(nseq - 1).wait()
-    for i in range(1, SLOTS):
-        wstart(i // 3, i % 3)
-    scopy(0).start()
-    scopy(1).start()
     lax.fori_loop(0, nseq, ln_body, 0)
 
     step_i = lax.broadcasted_iota(jnp.int32, (clen, clen), 0)
@@ -256,15 +263,16 @@
     rows, d_model = x2d.shape
     nseq, heads = state.shape[:2]
     clen = rows // nseq
-    smem = pl.BlockSpec(memory_space=pltpu.SMEM)
     anyspec = pl.BlockSpec(memory_space=pl.ANY)
-    vspec = pl.BlockSpec(memory_space=pltpu.VMEM)
     return pl.pallas_call(
         mix_kernel,
         out_shape=(jax.ShapeDtypeStruct((rows, heads * 512), BF), jax.ShapeDtypeStruct(state.shape, F32)),
-        in_specs=[smem, smem, anyspec] + [vspec] * 5 + [anyspec] * 5,
+        in_specs=[anyspec] * 13,
         out_specs=(anyspec, anyspec),
         scratch_shapes=[
+            pltpu.SMEM(log_gammas.shape, F32), pltpu.SMEM(start_pos.shape, jnp.int32),
+            pltpu.VMEM((1, 128), F32), pltpu.VMEM((clen, 128), F32), pltpu.VMEM((clen, 128), F32),
+            pltpu.VMEM((1, d_model), F32), pltpu.VMEM((1, d_model), F32), pltpu.SemaphoreType.DMA((7,)),
             pltpu.VMEM((rows, 128), F32), pltpu.VMEM((rows, 128), F32),
             pltpu.VMEM((rows, d_model), BF), pltpu.VMEM((rows, d_model), BF),
             pltpu.VMEM((SLOTS, d_model, 512), BF),
@@ -285,8 +293,8 @@
 TN = 512
 
 
-def ffn_kernel(z_hbm, x_hbm, g_ref, b_ref, wo, wup, wdn, o_hbm,
-               zb, wa, wbb, ub, drv, xrv, h2, x1,
+def ffn_kernel(z_hbm, x_hbm, g_hbm, b_hbm, wo, wup, wdn, o_hbm,
+               g_ref, b_ref, gb_sem, zb, wa, wbb, ub, drv, xrv, h2, x1,
                zsem, x1sem, wosem, wupsem, wdnsem, ds_sem, dr_sem, xs_sem, xr_sem, hs_sem, hr_sem, ol_sem, os_sem, or_sem):
     tp = lax.axis_index('tp')
     core = lax.rem(tp, 2)
@@ -316,6 +324,9 @@
         wo_copy(n).start()
         return carry
     lax.fori_loop(0, nt, start_wo, 0)
+    gain_copies = (pltpu.make_async_copy(g_hbm, g_ref, gb_sem.at[0]), pltpu.make_async_copy(b_hbm, b_ref, gb_sem.at[1]))
+    for copy in gain_copies:
+        copy.start(priority=1)
     x1_copy(0).start(priority=1)
     x1_copy(1).start(priority=1)
 
@@ -423,6 +434,8 @@
         for n in range(nt - lag, nt):
             forward(1, c, n)
 
+    for copy in gain_copies:
+        copy.wait()
     chunk(0)
     chunk(1)
 
@@ -467,14 +480,14 @@
     ku = fdim // 256
     hr = rows // 4
     anyspec = pl.BlockSpec(memory_space=pl.ANY)
-    vspec = pl.BlockSpec(memory_space=pltpu.VMEM)
     dma = pltpu.SemaphoreType.DMA
     return pl.pallas_call(
         ffn_kernel,
         out_shape=jax.ShapeDtypeStruct((rows, d_model), BF),
-        in_specs=[anyspec, anyspec, vspec, vspec, anyspec, anyspec, anyspec],
+        in_specs=[anyspec] * 7,
         out_specs=anyspec,
         scratch_shapes=[
+            pltpu.VMEM((1, d_model), F32), pltpu.VMEM((1, d_model), F32), dma((2,)),
             pltpu.VMEM((rows, width), BF),
             pltpu.VMEM((ku, d_model, 256), BF),
             pltpu.VMEM((nt, width, TN), BF),
@@ -493,6 +506,30 @@
     )(z2d, x2d, gain, bias, w_o, w_up, w_down)
 
 
+def emit_kernel(src, dst, buf, in_sem, out_sem):
+    parts = buf.shape[0]
+    ins = [pltpu.make_async_copy(src.at[i], buf.at[i], in_sem.at[i]) for i in range(parts)]
+    outs = [pltpu.make_async_copy(buf.at[i], dst.at[i], out_sem.at[i]) for i in range(parts)]
+    for copy in ins:
+        copy.start()
+    for copy_in, copy_out in zip(ins, outs):
+        copy_in.wait()
+        copy_out.start()
+    for copy in outs:
+        copy.wait()
+
+
+def emit_call(out):
+    dma = pltpu.SemaphoreType.DMA
+    anyspec = pl.BlockSpec(memory_space=pl.ANY)
+    return pl.pallas_call(
+        emit_kernel, out_shape=jax.ShapeDtypeStruct(out.shape, out.dtype), in_specs=[anyspec], out_specs=anyspec,
+        scratch_shapes=[pltpu.VMEM(out.shape, out.dtype), dma((out.shape[0],)), dma((out.shape[0],))],
+        compiler_params=pltpu.CompilerParams(vmem_limit_bytes=60 * 1024 * 1024),
+        name='emit',
+    )(out)
+
+
 def solution(mesh):
     def local_layer(x_in, start_pos, kv_state, ln1_gain, ln1_bias, w_q, w_k, w_v, w_g, w_o, ln2_gain, ln2_bias, w_up, w_down):
         nseq, clen, d_model = x_in.shape
@@ -502,7 +539,7 @@
         z2d, new_state = mix_call(x2d, start_pos, ln1_gain.reshape(1, -1), ln1_bias.reshape(1, -1),
                                   w_q, w_k, w_v, w_g, kv_state, log_gammas)
         out = ffn_call(z2d, x2d, ln2_gain.reshape(1, -1), ln2_bias.reshape(1, -1), w_o, w_up, w_down)
-        return out.reshape(x_in.shape), new_state
+        return emit_call(out.reshape(16, -1, d_model)).reshape(x_in.shape), new_state
 
     in_specs = (P('dp', None, None), P('dp'), P('dp', 'tp', None, None), P(), P(), P(None, 'tp'), P(None, 'tp'), P(None, 'tp'), P(None, 'tp'), P('tp', None), P(), P(), P(None, 'tp'), P('tp', None))
     out_specs = (P('dp', None, None), P('dp', 'tp', None, None))

time: 109 us -> 107 us (0.982)
  local copies, waits for them, and re-layouts: 3.4 us -> 0 us
  Pallas kernels: 105 us -> 107 us
    unnamed x1 -> x0, local copies, waits for them, and re-layouts: 3.4 us -> none
    pallas_call x0 -> x1, Pallas kernels: none -> 2.78 us  [emit_call(): pl.pallas_call(emit_kernel, out_shape=jax.ShapeDtypeStruct(out.shape, out...]
where the time goes in v4:
time: 107 us
  Pallas kernels  107 us (100%)
    pallas_call x1, Pallas kernels, ffn_call(): pl.pallas_call(ffn_kernel, out_shape=jax.ShapeDtypeStruct((rows, d_model)...  67.8 us
    pallas_call x1, Pallas kernels, mix_call(): pl.pallas_call(mix_kernel, out_shape=(jax.ShapeDtypeStruct((rows, heads *...  36.1 us
    pallas_call x1, Pallas kernels, emit_call(): pl.pallas_call(emit_kernel, out_shape=jax.ShapeDtypeStruct(out.shape, out...  2.78 us

profile of v4, /device:TPU:0, one launch (start us, length us, event | category | flops | bytes accessed | tf_op | source)
XLA Modules:
  0.0 107.3 jit_solution(13974303121635809614)
XLA Ops:
  0.6 36.1 %mix.1 = (bf16[256,2560]{1,0:T(8,128)(2,1)}, f32[4,5,256,512]{3,2,1,0:T(8,128)}) custom-call(f32[20]{0:T(128)} %constant.8.clone.lg_hbm, s32[4]{0:T(128)} %pos_hbm.1, bf16[256,5120]{1,0:T(8,128)(2,1)} %bitcast.7, f32[1,128]{1,0:T(1,128)} %constant.9.clone.freq_hbm, f32[64,128]{1,0:T(8,128)} %constant.10.clone.stepc_hbm, f32[64,128]{1,0:T(8,128)} %constant.11.clone.steps_hbm, ...), custom_call_target="tpu_custom_call" | custom-call | flops 20999999488 | bytes 102000000 | tf_op jit(solution)/shard_map/mix/pallas_call | solution.py:267
  36.7 67.8 %ffn.1 = bf16[256,5120]{1,0:T(8,128)(2,1)} custom-call(bf16[256,2560]{1,0:T(8,128)(2,1)} %get-tuple-element.4.z_hbm, bf16[256,5120]{1,0:T(8,128)(2,1)} %bitcast.8, f32[1,5120]{1,0:T(1,128)} %bitcast.13, f32[1,5120]{1,0:T(1,128)} %bitcast.14, bf16[2560,5120]{1,0:T(8,128)(2,1)} %wo.1, bf16[5120,2560]{1,0:T(8,128)(2,1)} %wup.1, bf16[2560,5120]{1,0:T(8,128)(2,1)} %wdn.1), custom_call_target="tpu_custom_call" | custom-call | flops 20000000000 | bytes 85000000 | tf_op jit(solution)/shard_map/ffn/pallas_call | solution.py:484
  104.5 2.8 %emit.1 = bf16[16,16,5120]{2,1,0:T(8,128)(2,1)} custom-call(bf16[16,16,5120]{2,1,0:T(8,128)(2,1)} %bitcast.9), custom_call_target="tpu_custom_call" | custom-call | tf_op jit(solution)/shard_map/emit/pallas_call | solution.py:525

commit v5 on v4

--- a/solution.py
+++ b/solution.py
@@ -78,9 +78,13 @@
         slot = lax.rem(head, 2)
         return pltpu.make_async_copy(s_hbm.at[:, head], sb.at[slot], ssem.at[slot])
 
-    def socopy(head):
+    def socopy(head, s):
         slot = lax.rem(head, 2)
-        return pltpu.make_async_copy(sob.at[slot], so_hbm.at[:, head], sosem.at[slot])
+        return pltpu.make_async_copy(sob.at[slot, s], so_hbm.at[s, head], sosem.at[slot, s])
+
+    def so_wait(head):
+        for s in range(nseq):
+            socopy(head, s).wait()
 
     def zcopy(head):
         slot = lax.rem(head, 2)
@@ -183,7 +187,7 @@
             high, low = split2(scores[s] * inner_decay)
             scb[s] = jnp.concatenate([high, low], axis=-1)
 
-    def ret_out(head, slot):
+    def ret_out(head, slot, early=False):
         log_g = lg_ref[first_head + head]
         query_decay = jnp.exp((tok_q + 1.0) * log_g)
         state_decay = jnp.exp(jnp.full((1, 512), clen, F32) * log_g)
@@ -192,6 +196,8 @@
             ob[seq_rows(s), :] = dot(scb[s], vb[slot, s]) + (dot(q, sth[s]) + dot(q, stl[s])) * query_decay
             update = lax.dot_general(kdb[s], vb[slot, s], (((0,), (0,)), ((), ())), preferred_element_type=F32)
             sob[slot, s] = sb[slot, s] * state_decay + update
+            if early:
+                socopy(head, s).start()
 
     def ret_gate(slot):
         for s in range(nseq):
@@ -220,7 +226,7 @@
 
         @pl.when(prev >= 2)
         def _():
-            socopy(prev - 2).wait()
+            so_wait(prev - 2)
             zcopy(prev - 2).wait()
         wwait(head, 0)
         scores = ret_scores(old)
@@ -231,7 +237,8 @@
         ret_out(prev, old)
         proj_v(head, slot)
         wnext(head, 1)
-        socopy(prev).start()
+        for s in range(nseq):
+            socopy(prev, s).start()
 
         @pl.when(head + 1 < heads)
         def _():
@@ -247,15 +254,14 @@
     last = heads - 1
     slot = last % 2
     scopy(last).wait()
-    socopy(last - 2).wait()
+    so_wait(last - 2)
     zcopy(last - 2).wait()
     ret_prepare(last, slot, ret_scores(slot))
-    ret_out(last, slot)
-    socopy(last).start()
+    ret_out(last, slot, early=True)
     ret_gate(slot)
     zcopy(last).start()
     for head in (last - 1, last):
-        socopy(head).wait()
+        so_wait(head)
         zcopy(head).wait()
 
 
@@ -282,7 +288,7 @@
             pltpu.VMEM((nseq, clen, 2 * clen), BF), pltpu.VMEM((nseq, 256, 512), BF), pltpu.VMEM((nseq, 256, 512), BF),
             pltpu.VMEM((nseq, 2 * clen, 256), BF), pltpu.VMEM((rows, 512), F32), pltpu.VMEM((2, rows, 512), BF),
             pltpu.SemaphoreType.DMA((nseq,)), pltpu.SemaphoreType.DMA((SLOTS, 2)), pltpu.SemaphoreType.DMA((2,)),
-            pltpu.SemaphoreType.DMA((2,)), pltpu.SemaphoreType.DMA((2,)),
+            pltpu.SemaphoreType.DMA((2, nseq)), pltpu.SemaphoreType.DMA((2,)),
         ],
         compiler_params=pltpu.CompilerParams(vmem_limit_bytes=60 * 1024 * 1024),
         cost_estimate=pl.CostEstimate(flops=21_000_000_000, bytes_accessed=102_000_000, transcendentals=0),
@@ -539,7 +545,7 @@
         z2d, new_state = mix_call(x2d, start_pos, ln1_gain.reshape(1, -1), ln1_bias.reshape(1, -1),
                                   w_q, w_k, w_v, w_g, kv_state, log_gammas)
         out = ffn_call(z2d, x2d, ln2_gain.reshape(1, -1), ln2_bias.reshape(1, -1), w_o, w_up, w_down)
-        return emit_call(out.reshape(16, -1, d_model)).reshape(x_in.shape), new_state
+        return emit_call(out.reshape(8, -1, d_model)).reshape(x_in.shape), new_state
 
     in_specs = (P('dp', None, None), P('dp'), P('dp', 'tp', None, None), P(), P(), P(None, 'tp'), P(None, 'tp'), P(None, 'tp'), P(None, 'tp'), P('tp', None), P(), P(), P(None, 'tp'), P('tp', None))
     out_specs = (P('dp', None, None), P('dp', 'tp', None, None))

time: 107 us -> 107 us (level)
  no operation moved by 1% of the time
where the time goes in v5:
time: 107 us
  Pallas kernels  106 us (99%)
    pallas_call x1, Pallas kernels, ffn_call(): pl.pallas_call(ffn_kernel, out_shape=jax.ShapeDtypeStruct((rows, d_model)...  67.8 us
    pallas_call x1, Pallas kernels, mix_call(): pl.pallas_call(mix_kernel, out_shape=(jax.ShapeDtypeStruct((rows, heads *...  35.6 us
    pallas_call x1, Pallas kernels, emit_call(): pl.pallas_call(emit_kernel, out_shape=jax.ShapeDtypeStruct(out.shape, out...  2.59 us

profile of v5, /device:TPU:0, one launch (start us, length us, event | category | flops | bytes accessed | tf_op | source)
XLA Modules:
  0.0 106.6 jit_solution(17932272521652819223)
XLA Ops:
  0.6 35.6 %mix.1 = (bf16[256,2560]{1,0:T(8,128)(2,1)}, f32[4,5,256,512]{3,2,1,0:T(8,128)}) custom-call(f32[20]{0:T(128)} %constant.8.clone.lg_hbm, s32[4]{0:T(128)} %pos_hbm.1, bf16[256,5120]{1,0:T(8,128)(2,1)} %bitcast.7, f32[1,128]{1,0:T(1,128)} %constant.9.clone.freq_hbm, f32[64,128]{1,0:T(8,128)} %constant.10.clone.stepc_hbm, f32[64,128]{1,0:T(8,128)} %constant.11.clone.steps_hbm, ...), custom_call_target="tpu_custom_call" | custom-call | flops 20999999488 | bytes 102000000 | tf_op jit(solution)/shard_map/mix/pallas_call | solution.py:273
  36.2 67.8 %ffn.1 = bf16[256,5120]{1,0:T(8,128)(2,1)} custom-call(bf16[256,2560]{1,0:T(8,128)(2,1)} %get-tuple-element.4.z_hbm, bf16[256,5120]{1,0:T(8,128)(2,1)} %bitcast.8, f32[1,5120]{1,0:T(1,128)} %bitcast.13, f32[1,5120]{1,0:T(1,128)} %bitcast.14, bf16[2560,5120]{1,0:T(8,128)(2,1)} %wo.1, bf16[5120,2560]{1,0:T(8,128)(2,1)} %wup.1, bf16[2560,5120]{1,0:T(8,128)(2,1)} %wdn.1), custom_call_target="tpu_custom_call" | custom-call | flops 20000000000 | bytes 85000000 | tf_op jit(solution)/shard_map/ffn/pallas_call | solution.py:490
  104.0 2.6 %emit.1 = bf16[8,32,5120]{2,1,0:T(8,128)(2,1)} custom-call(bf16[8,32,5120]{2,1,0:T(8,128)(2,1)} %bitcast.9), custom_call_target="tpu_custom_call" | custom-call | tf_op jit(solution)/shard_map/emit/pallas_call | solution.py:531
